TPU v7x, 8 devices: a whole 2x2x1 slice. The times are simulated.
8 devices in a mesh: slab: 1 (over z), coil: 2 (over y), rows: 4 (over x, core).
Axes of the slice: x: 2, y: 2, z: 1, core: 2. Of those that a mesh axis runs over, the one named last changes fastest.
Arguments:
- kspace: float32 [2, 8, 8192], P(None, 'coil', ('slab', 'rows'))
- weight_row: float32 [6, 8192], P(None, ('slab', 'rows'))
- weight_col: float32 [6, 8192], P(None, ('slab', 'rows'))
- grid_row: int32 [8192], P(('slab', 'rows'))
- grid_col: int32 [8192], P(('slab', 'rows'))
- valid_count: int32 [4], P(('slab', 'rows'))
- coil_maps: float32 [2, 8, 512, 512], P(None, 'coil', 'slab', 'rows')
- deapod: float32 [512], replicated
Outputs:
- output: float32 [2, 512, 512], P(None, ('slab', 'coil'), 'rows')
All inputs are finite; a program needn't handle non-finite values.
Results may differ from a plain program's by a relative error of at most 0.001.
Values are sent between devices in bfloat16 or wider.
A program may use at most 1 GiB of HBM per device.

v0:
```python
import math
import jax
import jax.numpy as jnp
from jax import lax
from jax.sharding import PartitionSpec as P


def make_table(n_img):
    n_grid = 2 * n_img
    freq_index = jnp.arange(n_grid, dtype=jnp.int32) - n_img
    pixel_index = jnp.arange(n_img, dtype=jnp.int32) - n_img // 2
    angle_grid = jnp.mod(freq_index[:, None] * pixel_index[None, :], n_grid).astype(jnp.float32) * (2.0 * math.pi / n_grid)
    cos_part = jnp.cos(angle_grid)
    sin_part = jnp.sin(angle_grid)
    return jnp.stack([jnp.stack([cos_part, sin_part], axis=1), jnp.stack([-sin_part, cos_part], axis=1)], axis=0).astype(jnp.bfloat16)


def spread_block(kspace, weight_row, weight_col, grid_row, grid_col, valid_count, first_row, buf_rows, n_grid):
    width = weight_row.shape[0]
    half_width = width // 2
    samples = kspace.shape[2]
    zero_bf = jnp.zeros((), jnp.bfloat16)
    keep_mask = (jnp.arange(samples) < valid_count[0]).astype(jnp.float32)
    row_coef = (kspace[:, :, None, :] * (weight_row * keep_mask)[None, None, :, :]).astype(jnp.bfloat16)
    kernel_idx = jnp.arange(width)
    row_offset = jnp.arange(buf_rows)[:, None] - (grid_row - first_row)[None, :]
    left_side = jnp.sum(jnp.where(row_offset[None, None, None] == kernel_idx[None, None, :, None, None], row_coef[:, :, :, None, :], zero_bf), axis=2)
    col_offset = jnp.mod(jnp.arange(n_grid)[None, :] - grid_col[:, None] + half_width, n_grid)
    right_side = jnp.sum(jnp.where(col_offset[None] == kernel_idx[:, None, None], weight_col.astype(jnp.bfloat16)[:, :, None], zero_bf), axis=0)
    return jnp.einsum('qcrm,mk->qcrk', left_side, right_side, preferred_element_type=jnp.float32)


def solution(mesh):
    n_rows = mesh.shape['rows']
    to_prev = [(index, (index - 1) % n_rows) for index in range(n_rows)]
    to_next = [(index, (index + 1) % n_rows) for index in range(n_rows)]

    def local_part(kspace, weight_row, weight_col, grid_row, grid_col, valid_count, coil_maps, deapod):
        n_img = deapod.shape[0]
        n_grid = 2 * n_img
        block_rows = n_grid // n_rows
        half_width = weight_row.shape[0] // 2
        row_id = lax.axis_index('rows')
        block_grid = spread_block(kspace, weight_row, weight_col, grid_row, grid_col, valid_count, row_id * block_rows, block_rows + 2 * half_width, n_grid)
        from_next = lax.ppermute(block_grid[:, :, :half_width], 'rows', to_prev)
        from_prev = lax.ppermute(block_grid[:, :, block_rows + half_width:], 'rows', to_next)
        own_rows = block_grid[:, :, half_width:half_width + block_rows]
        summed = jnp.concatenate([own_rows[:, :, :half_width] + from_prev, own_rows[:, :, half_width:block_rows - half_width], own_rows[:, :, block_rows - half_width:] + from_next], axis=2).astype(jnp.bfloat16)
        dft_table = make_table(n_img)
        half_image = jnp.einsum('qcrk,qkbj->bcrj', summed, dft_table, preferred_element_type=jnp.float32).astype(jnp.bfloat16)
        columns = lax.all_to_all(half_image, 'rows', 3, 2, tiled=True)
        coil_image = jnp.einsum('bcyj,byei->ecij', columns, dft_table, preferred_element_type=jnp.float32)
        real_part = jnp.sum(coil_maps[0] * coil_image[0] + coil_maps[1] * coil_image[1], axis=0)
        imag_part = jnp.sum(coil_maps[0] * coil_image[1] - coil_maps[1] * coil_image[0], axis=0)
        combined = lax.psum_scatter(jnp.stack([real_part, imag_part]), 'coil', scatter_dimension=1, tiled=True)
        out_rows = combined.shape[1]
        out_cols = combined.shape[2]
        row_scale = lax.dynamic_slice_in_dim(deapod, lax.axis_index('coil') * out_rows, out_rows)
        col_scale = lax.dynamic_slice_in_dim(deapod, row_id * out_cols, out_cols)
        return combined * (row_scale[:, None] * col_scale[None, :])[None]

    spec_samples = P(None, 'coil', ('slab', 'rows'))
    spec_weights = P(None, ('slab', 'rows'))
    spec_index = P(('slab', 'rows'))
    return jax.shard_map(local_part, mesh=mesh, in_specs=(spec_samples, spec_weights, spec_weights, spec_index, spec_index, spec_index, P(None, 'coil', 'slab', 'rows'), P()), out_specs=P(None, ('slab', 'coil'), 'rows'), check_vma=False)
```

profile of v0, /device:TPU:0, one launch (start us, length us, event | category | flops | bytes accessed | tf_op | source)
XLA Modules:
  0.0 190.4 jit_solution(4130413168987065576)
XLA Ops:
  6.5 0.0 copy-start.6
  6.5 0.0 reduce-scatter.2.cloned.1.call-start
  6.5 0.7 broadcast_subtract_fusion
  7.3 0.2 iota_subtract_fusion
  7.5 1.9 %iota_compare_fusion.1 = pred[6,262,2048]{2,1,0:T(8,128)(4,1)S(1)} fusion(s32[262,2048]{1,0:T(8,128)S(1)} %iota_subtract_fusion), kind=kLoop, calls=%fused_computation.4 | loop fusion | flops 3219456 | bytes 5365760 | tf_op jit(solution)/shard_map/eq | solution.py:27
  10.1 0.0 copy-done.6
  10.1 0.0 copy-start.4
  10.1 0.0 copy-start.5
  10.2 0.0 copy-start.3
  10.2 5.8 %add_select_fusion = s32[2048,1024]{1,0:T(8,128)} fusion(s32[2048]{0:T(1024)S(1)} %copy-done.6), kind=kLoop, calls=%fused_computation.5 | loop fusion | flops 27262976 | bytes 8396800 | tf_op jit(solution)/shard_map/jit(remainder)/select_n | solution.py:28
  16.0 0.0 copy-done.4
  16.0 0.0 copy-done.5
  16.0 0.0 copy-done.3
  16.0 0.1 multiply_convert_fusion
  16.1 61.6 %select_reduce_fusion = bf16[2,4,262,2048]{3,1,2,0:T(4,128)(2,1)} fusion(pred[6,262,2048]{2,1,0:T(8,128)(4,1)S(1)} %iota_compare_fusion.1, bf16[2,4,6,2048]{3,1,2,0:T(4,128)(2,1)S(1)} %multiply_convert_fusion), kind=kLoop, calls=%fused_computation | loop fusion | flops 47218688 | bytes 12001280 | tf_op jit(solution)/shard_map/reduce_sum | solution.py:27
  77.7 11.9 %fusion.1 = bf16[2048,1024]{1,0:T(8,128)(2,1)} fusion(s32[2048,1024]{1,0:T(8,128)} %add_select_fusion, bf16[6,2048]{1,0:T(8,128)(2,1)S(1)} %convert_element_type.56), kind=kLoop, calls=%fused_computation.3 | loop fusion | flops 35651584 | bytes 12607488 | tf_op jit(solution)/shard_map/reduce_sum | solution.py:29
  89.6 20.6 %fusion.2 = f32[2,4,262,1024]{3,2,1,0:T(8,128)S(1)} fusion(bf16[2,4,262,2048]{3,1,2,0:T(4,128)(2,1)} %select_reduce_fusion, bf16[2048,1024]{1,0:T(8,128)(2,1)} %fusion.1), kind=kOutput, calls=%fused_computation.8 | convolution fusion | flops 8791261184 | bytes 21364736 | tf_op jit(solution)/shard_map/qcrm,mk->qcrk/dot_general | solution.py:30
  110.3 0.9 collective-permute-start
  111.2 9.3 %fusion.18 = (bf16[1024,1,512]{0,2,1:T(8,128)(2,1)S(1)}, bf16[1024,1,512]{0,2,1:T(8,128)(2,1)S(1)}, bf16[1024,1,512]{0,2,1:T(8,128)(2,1)S(1)}) fusion(s32[512]{0:T(512)S(1)} %iota_add_fusion.1, s32[1024]{0:T(1024)S(1)} %iota_add_fusion), kind=kLoop, calls=%fused_computation.38 | loop fusion | flops 9437184 | bytes 3151872 | tf_op jit(solution)/shard_map/convert.13
  120.4 0.0 collective-permute-done
  120.5 0.1 fusion.20
  120.5 2.0 %collective-permute-start.1 = (f32[2,4,3,1024]{3,2,1,0:T(4,128)S(1)}, f32[2,4,3,1024]{3,2,1,0:T(4,128)S(1)}, u32[]{:S(2)}, u32[]{:S(2)}) collective-permute-start(f32[2,4,3,1024]{3,2,1,0:T(4,128)S(1)} %get-tuple-element.8), channel_id=1, source_target_pairs={{0,3},{1,0},{2,1},{3,2},{4,7},{5,4},{6,5},{7,6}} | collective-permute-start | bytes 294920 | tf_op jit(solution)/shard_map/ppermute | solution.py:45
  122.5 0.4 maximum_bitcast_fusion.3
  122.9 0.0 copy-start
  122.9 0.0 copy-start.1
  122.9 1.4 slice.67
  124.3 0.7 collective-permute-done.1
  125.1 0.0 copy-done
  125.1 0.0 copy-done.1
  125.1 4.5 %fusion.13 = bf16[2,4,256,512]{2,3,1,0:T(8,128)(2,1)S(1)} fusion(bf16[1,1024,2,512]{1,3,0,2:T(8,128)(2,1)S(1)} %get-tuple-element.10, bf16[1,1024,2,512]{1,3,0,2:T(8,128)(2,1)S(1)} %get-tuple-element.9, bf16[2,4,3,1024]{3,2,1,0:T(4,128)(2,1)S(1)} %fusion.19, bf16[2,4,250,1024]{3,2,1,0:T(8,128)(2,1)S(1)} %slice.67, ...), kind=kOutput, calls=%fused_computation.29 | convolution fusion | flops 4316987392 | bytes 10485760 | tf_op jit(solution)/shard_map/qcrk,qkbj->bcrj/dot_general | solution.py:50
  129.6 1.6 copy.19
  131.3 29.2 %all_to_all.18 = bf16[2,4,256,512]{2,1,0,3:T(4,128)(2,1)S(1)} all-to-all(bf16[2,4,256,512]{2,1,0,3:T(4,128)(2,1)S(1)} %copy.19), channel_id=1, replica_groups=mesh['slab'=1,'coil'=2,'rows'=4] {'rows'}, dimensions={3} | all-to-all | bytes 4194304 | tf_op jit(solution)/shard_map/all_to_all | solution.py:51
  160.5 2.7 %copy.20 = bf16[2,4,256,4,128]{4,2,3,0,1:T(8,128)(2,1)} copy(bf16[2,4,256,4,128]{2,1,0,4,3:T(4,128)(2,1)S(1)} %bitcast.49) | data formatting | bytes 4194304 | tf_op jit(solution)/shard_map/all_to_all | solution.py:51
  163.2 0.0 copy-start.2
  163.2 5.3 %fusion.16 = f32[2,4,512,128]{3,2,1,0:T(8,128)S(1)} fusion(bf16[2,4,1024,128,1]{3,2,0,1,4:T(8,128)(2,1)} %bitcast.50, bf16[1,1024,2,512]{1,3,0,2:T(8,128)(2,1)} %copy-done.1, bf16[1,1024,2,512]{1,3,0,2:T(8,128)(2,1)} %copy-done), kind=kOutput, calls=%fused_computation.34 | convolution fusion | flops 2155872256 | bytes 8388608 | tf_op jit(solution)/shard_map/bcyj,byei->ecij/dot_general | solution.py:52
  168.6 0.0 copy-done.2
  168.6 0.0 copy-start.7
  168.6 0.4 add_reduce_fusion
  169.0 0.8 pad_maximum_fusion.1
  169.8 0.0 reduce-scatter.2.cloned.1.call-update
  169.8 0.0 copy-done.7
  169.8 0.1 dynamic_slice.7
  169.9 0.1 dynamic_slice.6
  170.0 0.1 broadcast_multiply_fusion.1
  170.1 11.8 %reduce-scatter.2.cloned.1.call-done = f32[2,256,128]{2,1,0:T(8,128)} async-done(((f32[2,512,128]{2,1,0:T(8,128)}), f32[2,256,128]{2,1,0:T(8,128)}) %reduce-scatter.2.cloned.1.call-update) | async-done | bytes 262160 | tf_op jit(solution)/shard_map/reduce_scatter | solution.py:55
  181.9 1.7 broadcast_multiply_fusion
  (7 shorter events, 0.1 us)
Async XLA Ops:
  6.5 3.6 %copy-start.6 = (s32[2048]{0:T(1024)S(1)}, s32[2048]{0:T(1024)}, u32[]{:S(2)}) copy-start(s32[2048]{0:T(1024)} %param.12) | copy-start | bytes 24580
  6.5 175.4 %reduce-scatter.2.cloned.1.call-start = ((), (), s32[]{:S(2)}) async-start(), calls=%async_computation.2 | async-start | bytes 786432 | tf_op jit(solution)/shard_map/reduce_scatter | solution.py:55
  10.1 5.8 %copy-start.4 = (f32[6,2048]{1,0:T(8,128)S(1)}, f32[6,2048]{1,0:T(8,128)}, u32[]{:S(2)}) copy-start(f32[6,2048]{1,0:T(8,128)} %param.10) | copy-start | bytes 147460
  10.1 5.8 %copy-start.5 = (f32[6,2048]{1,0:T(8,128)S(1)}, f32[6,2048]{1,0:T(8,128)}, u32[]{:S(2)}) copy-start(f32[6,2048]{1,0:T(8,128)} %param.9) | copy-start | bytes 147460
  10.2 5.8 %copy-start.3 = (f32[2,4,2048]{2,1,0:T(4,128)S(1)}, f32[2,4,2048]{2,1,0:T(4,128)}, u32[]{:S(2)}) copy-start(f32[2,4,2048]{2,1,0:T(4,128)} %param.8) | copy-start | bytes 196612
  110.3 10.2 %collective-permute-start = (f32[2,4,3,1024]{3,2,1,0:T(4,128)S(1)}, f32[2,4,3,1024]{3,2,1,0:T(4,128)S(1)}, u32[]{:S(2)}, u32[]{:S(2)}) collective-permute-start(f32[2,4,3,1024]{3,2,1,0:T(4,128)S(1)} %slice.46), channel_id=1, source_target_pairs={{0,1},{1,2},{2,3},{3,0},{4,5},{5,6},{6,7},{7,4}} | collective-permute-start | bytes 294920 | tf_op jit(solution)/shard_map/ppermute | solution.py:46
  120.5 4.5 %collective-permute-start.1 = (f32[2,4,3,1024]{3,2,1,0:T(4,128)S(1)}, f32[2,4,3,1024]{3,2,1,0:T(4,128)S(1)}, u32[]{:S(2)}, u32[]{:S(2)}) collective-permute-start(f32[2,4,3,1024]{3,2,1,0:T(4,128)S(1)} %get-tuple-element.8), channel_id=1, source_target_pairs={{0,3},{1,0},{2,1},{3,2},{4,7},{5,4},{6,5},{7,6}} | collective-permute-start | bytes 294920 | tf_op jit(solution)/shard_map/ppermute | solution.py:45
  122.9 2.2 %copy-start = (bf16[1,1024,2,512]{1,3,0,2:T(8,128)(2,1)}, bf16[1,1024,2,512]{1,3,0,2:T(8,128)(2,1)S(1)}, u32[]{:S(2)}) copy-start(bf16[1,1024,2,512]{1,3,0,2:T(8,128)(2,1)S(1)} %get-tuple-element.9) | copy-start | bytes 6291460
  122.9 2.2 %copy-start.1 = (bf16[1,1024,2,512]{1,3,0,2:T(8,128)(2,1)}, bf16[1,1024,2,512]{1,3,0,2:T(8,128)(2,1)S(1)}, u32[]{:S(2)}) copy-start(bf16[1,1024,2,512]{1,3,0,2:T(8,128)(2,1)S(1)} %get-tuple-element.10) | copy-start | bytes 6291460
  163.2 5.3 %copy-start.2 = (f32[2,4,512,128]{3,2,1,0:T(8,128)S(1)}, f32[2,4,512,128]{3,2,1,0:T(8,128)}, u32[]{:S(2)}) copy-start(f32[2,4,512,128]{3,2,1,0:T(8,128)} %param.14) | copy-start | bytes 6291460
  168.6 1.2 copy-start.7
Sparse Core Ops, SparseCore 0:
  169.9 11.9 reduce-scatter.1
where the time goes:
time: 191 us; the launch traced here: 190 us
  other arithmetic  95 us (50%)
  matrix products  30.5 us (16%)
  blocking collectives  29.2 us (15%)
  between operations  14.3 us (7%)
  waiting for transfers between devices  12.6 us (7%)
  local copies, waits for them, and re-layouts  5.98 us (3%)
  starting transfers between devices  2.88 us (2%)
    reduce_sum x1, other arithmetic, spread_block(): jnp.sum(jnp.where(row_offset[None, None, None] == kernel_idx[None, None,...  61.6 us
    all_to_all x1, blocking collectives, local_part(): columns = lax.all_to_all(half_image, 'rows', 3, 2, tiled=True)  29.2 us
    dot_general x1, matrix products, spread_block(): jnp.einsum('qcrm,mk->qcrk', left_side, right_side, preferred_element_type...  20.6 us
    reduce_sum x1, other arithmetic, spread_block(): jnp.sum(jnp.where(col_offset[None] == kernel_idx[:, None, None], weight_c...  11.9 us
    reduce_scatter x1, waiting for transfers between devices, local_part(): lax.psum_scatter(jnp.stack([real_part, imag_part]), 'coil', scatter_dimen...  11.8 us
    another operation x3, other arithmetic  9.35 us
    select_n x1, other arithmetic, spread_block(): jnp.mod(jnp.arange(n_grid)[None, :] - grid_col[:, None] + half_width, n_g...  5.79 us
    dot_general x1, matrix products, local_part(): jnp.einsum('bcyj,byei->ecij', columns, dft_table, preferred_element_type=...  5.32 us
  transfers between devices with their start and end apart: 3, of which 2 were waited for; matrix products, arithmetic and copies ran while one was open for 6% of the time, Pallas kernels for 0%

commit v1 on v0

v1 whole, which is shorter than its diff:
```python
import math
import functools
import numpy as np
import jax
import jax.numpy as jnp
from jax import lax
from jax.experimental import pallas as pl
from jax.experimental.pallas import tpu as pltpu
from jax.sharding import PartitionSpec as P

F32 = jnp.float32
BF = jnp.bfloat16
NT = (((1,), (1,)), ((), ()))
KC = 512


def tables(n_img):
    n_grid = 2 * n_img
    pix = np.arange(n_img) - n_img // 2
    freq = np.arange(n_grid) - n_img
    ang = np.mod(pix[:, None] * freq[None, :], n_grid) * (2.0 * math.pi / n_grid)
    return np.stack([np.cos(ang), np.sin(ang)]).astype(np.float32).astype(BF)


def spread_kernel(pk, tab, h_ref, e_ref, acc, a_buf, b_buf, g_buf, hs, t_buf, sem):
    n_grid = 1024
    x_id = lax.axis_index('rows') // 2
    my_cols = pl.ds(pl.multiple_of(x_id * 256, 256), 256)
    copies = [
        pltpu.make_async_copy(tab.at[0, my_cols], t_buf.at[0, :, pl.ds(0, n_grid)], sem.at[0]),
        pltpu.make_async_copy(tab.at[1, my_cols], t_buf.at[1, :, pl.ds(0, n_grid)], sem.at[1]),
        pltpu.make_async_copy(tab.at[0, my_cols], t_buf.at[1, :, pl.ds(n_grid, n_grid)], sem.at[2]),
    ]
    for cp in copies:
        cp.start()
    valid = jnp.max(pk[22:23, 0:128]).astype(jnp.int32)
    n_chunk = (valid + (KC - 1)) // KC

    def build(s):
        cols = pl.ds(pl.multiple_of(s * KC, KC), KC)
        sub = lax.broadcasted_iota(jnp.int32, (16, KC), 0)
        keep = (lax.broadcasted_iota(jnp.int32, (1, KC), 1) + s * KC) < valid
        r0 = pk[20:21, cols].astype(jnp.int32) + 1
        u = jnp.broadcast_to((r0 >> 2).astype(F32), (16, KC)).astype(BF)
        t = (sub >> 2) - (r0 & 3)
        es = []
        for q in range(2):
            y16 = jnp.zeros((16, KC), F32)
            for c in range(4):
                y16 = jnp.where((sub & 3) == c, pk[4 * q + c:4 * q + c + 1, cols], y16)
            coef = [jnp.where(keep, y16 * pk[8 + a:9 + a, cols], 0.0) for a in range(6)]
            row = []
            for j in range(3):
                e = jnp.zeros((16, KC), F32)
                for a in range(6):
                    if -3 <= a - 4 * j <= 3:
                        e = jnp.where(t == a - 4 * j, coef[a], e)
                row.append(e.astype(BF))
            es.append(row)
        zero = jnp.zeros((16, KC), BF)
        for g in range(66):
            m0 = u == jnp.array(g, BF)
            m1 = u == jnp.array(g - 1, BF)
            m2 = u == jnp.array(g - 2, BF)
            for q in range(2):
                a_buf[1056 * q + 16 * g:1056 * q + 16 * g + 16, :] = jnp.where(m0, es[q][0], jnp.where(m1, es[q][1], jnp.where(m2, es[q][2], zero)))
        c0 = (pk[21:22, cols].astype(jnp.int32) + (n_grid - 3)) & (n_grid - 1)
        uc = jnp.broadcast_to((c0 >> 4).astype(F32), (16, KC)).astype(BF)
        tc = sub - (c0 & 15)
        eb = []
        for j in range(2):
            e = jnp.zeros((16, KC), F32)
            for b in range(6):
                e = jnp.where(tc == b - 16 * j, pk[14 + b:15 + b, cols], e)
            eb.append(e.astype(BF))
        for g in range(64):
            m0 = uc == jnp.array(g, BF)
            m1 = uc == jnp.array((g - 1) % 64, BF)
            b_buf[16 * g:16 * g + 16, :] = jnp.where(m0, eb[0], jnp.where(m1, eb[1], zero))

    def mults(first):
        @pl.loop(0, 2)
        def _(q):
            rows = pl.ds(pl.multiple_of(q * 1056, 16), 1056)
            prod = lax.dot_general(a_buf[rows, :], b_buf[...], NT, preferred_element_type=F32)
            if first:
                acc[rows, :] = prod
            else:
                acc[rows, :] += prod

    build(0)
    mults(True)

    @pl.loop(1, n_chunk)
    def _(s):
        build(s)
        mults(False)

    for cp in copies:
        cp.wait()
    t_buf[0, :, n_grid:] = -t_buf[1, :, :n_grid]
    for q in range(2):
        e_ref[q, 0:32] = acc[1056 * q:1056 * q + 32, :]
        e_ref[q, 32:64] = acc[1056 * q + 1024:1056 * q + 1056, :]
        g_buf[:, n_grid * q:n_grid * (q + 1)] = acc[1056 * q + 16:1056 * q + 1040, :].astype(BF)
    for e in range(2):
        prod = lax.dot_general(g_buf[...], t_buf[e], NT, preferred_element_type=F32)
        for hc in range(2):
            hs[2 * e + hc] = prod[:, 128 * hc:128 * hc + 128]
    for e in range(2):
        for hc in range(2):
            for c in range(4):
                h_ref[hc, e, :, 128 * c:128 * c + 128] = hs[2 * e + hc, pl.ds(c, 256, stride=4), :].astype(BF)


def spread(pk, tab):
    vm = pl.BlockSpec(memory_space=pltpu.VMEM)
    return pl.pallas_call(
        spread_kernel,
        out_shape=(jax.ShapeDtypeStruct((2, 2, 256, 512), BF), jax.ShapeDtypeStruct((2, 64, 1024), F32)),
        in_specs=[vm, pl.BlockSpec(memory_space=pl.ANY)],
        out_specs=(vm, vm),
        scratch_shapes=[
            pltpu.VMEM((2112, 1024), F32),
            pltpu.VMEM((2112, KC), BF),
            pltpu.VMEM((1024, KC), BF),
            pltpu.VMEM((1024, 2048), BF),
            pltpu.VMEM((4, 1024, 128), F32),
            pltpu.VMEM((2, 256, 2048), BF),
            pltpu.SemaphoreType.DMA((3,)),
        ],
        compiler_params=pltpu.CompilerParams(vmem_limit_bytes=40 * 2**20),
        cost_estimate=pl.CostEstimate(flops=13 * 10**9, bytes_accessed=4 * 2**20, transcendentals=0),
        name='spread',
    )(pk, tab)


def combine_kernel(h_own, h_nb, e_own, e_nb, tab, maps, out_ref,
                   t3, rhs, sbuf, s_vm, rx, ge, hs, pt, part, rx2,
                   loc, esend, erecv, hsend, hrecv, psend, precv, ysend, yrecv):
    n_grid = 1024
    row_id = lax.axis_index('rows')
    y_id = lax.axis_index('coil')
    core = row_id % 2
    x_id = row_id // 2
    sib = {'rows': row_id + 1 - 2 * core}
    mate = {'coil': 1 - y_id}
    blocks = [row_id, (row_id + 2) % 4]
    hh = [h_own, h_nb]
    ee = [e_own, e_nb]

    n_loc = 0
    t_copies = []
    for src, dst in ((tab.at[0], t3.at[0, :, pl.ds(0, n_grid)]), (tab.at[1], t3.at[1, :, pl.ds(0, n_grid)]), (tab.at[0], t3.at[1, :, pl.ds(n_grid, n_grid)])):
        t_copies.append(pltpu.make_async_copy(src, dst, loc.at[n_loc]))
        n_loc += 1
    h_copies = []
    for o in range(2):
        for b in range(2):
            h_copies.append(pltpu.make_async_copy(hh[o].at[core, b], rhs.at[b, blocks[o]], loc.at[n_loc]))
            n_loc += 1
            for end in range(2):
                h_copies.append(pltpu.make_async_copy(hh[o].at[1 - core, b, pl.ds(240 * end, 16)], sbuf.at[o, b, end], loc.at[n_loc]))
                n_loc += 1
    s_copy = pltpu.make_async_copy(maps, s_vm, loc.at[n_loc])
    for cp in t_copies + h_copies:
        cp.start()

    barrier = pltpu.get_barrier_semaphore()
    pl.semaphore_signal(barrier, inc=1, device_id=sib, device_id_type=pl.DeviceIdType.MESH)
    pl.semaphore_signal(barrier, inc=1, device_id=mate, device_id_type=pl.DeviceIdType.MESH)
    pl.semaphore_wait(barrier, 2)

    def remote(src, dst, ssem, rsem, dev):
        return pltpu.make_async_remote_copy(src_ref=src, dst_ref=dst, send_sem=ssem, recv_sem=rsem, device_id=dev, device_id_type=pl.DeviceIdType.MESH)

    e_copies = []
    for o in range(2):
        low = o * core + (1 - o) * (1 - core)
        high = o * (1 - core) + (1 - o) * core
        for k, (slot, end, row0) in enumerate(((low, 1, 0), (high, 0, 48))):
            e_copies.append(remote(ee[o].at[:, pl.ds(row0, 16)], rx.at[slot, end], esend.at[2 * o + k], erecv.at[slot, end], sib))
    for cp in e_copies:
        cp.start()
    hr_copies = []
    for o in range(2):
        for b in range(2):
            hr_copies.append(remote(hh[o].at[1 - core, b, pl.ds(16, 224)], rhs.at[b, blocks[o], pl.ds(16, 224)], hsend.at[o, b], hrecv.at[o, b], sib))
    for cp in hr_copies:
        cp.start()
    s_copy.start()

    for cp in t_copies:
        cp.wait()
    t3[0, :, n_grid:] = -t3[1, :, :n_grid]
    for cp in e_copies:
        cp.wait_send()
    for o in range(2):
        for end in range(2):
            remote(rx.at[o, end], rx.at[o, end], esend.at[2 * o + end], erecv.at[o, end], sib).wait_recv()
            for q in range(2):
                ge[32 * o + 16 * end:32 * o + 16 * end + 16, n_grid * q:n_grid * (q + 1)] = (ee[o][q, 16 + 16 * end:32 + 16 * end, :] + rx[o, end, q]).astype(BF)
    cols = pl.ds(pl.multiple_of(x_id * 256, 256), 256)
    for e in range(2):
        prod = lax.dot_general(ge[...], t3[e, cols, :], NT, preferred_element_type=F32)
        for hc in range(2):
            hs[2 * e + hc] = prod[:, 128 * hc:128 * hc + 128]
    for cp in h_copies:
        cp.wait()
    p_copies = []
    n_p = 0
    for o in range(2):
        for end in range(2):
            for b in range(2):
                for mine in range(2):
                    hc = core if mine else 1 - core
                    rows = pl.ds(240 * end, 16)
                    if mine:
                        pt[...] = rhs[b, blocks[o], rows, :].astype(F32)
                    else:
                        pt[...] = sbuf[o, b, end].astype(F32)
                    for c in range(4):
                        pt[12 * end:12 * end + 4, 128 * c:128 * c + 128] = hs[2 * b + hc, pl.ds(32 * o + 16 * end + c, 4, stride=4), :]
                    if mine:
                        rhs[b, blocks[o], rows, :] = pt[...].astype(BF)
                    else:
                        sbuf[o, b, end] = pt[...].astype(BF)
                        cp = remote(sbuf.at[o, b, end], rhs.at[b, blocks[o], rows], psend.at[n_p], precv.at[n_p], sib)
                        cp.start()
                        p_copies.append(cp)
                        n_p += 1
    s_copy.wait()
    for cp in hr_copies + p_copies:
        cp.wait()

    def image_rows(i0, size):
        rows = pl.ds(pl.multiple_of(i0, size), size)
        w = rhs[...].reshape(2048, 512)
        im = [jnp.dot(t3[e, rows, :], w, preferred_element_type=F32) for e in range(2)]
        xr = jnp.zeros((size, 128), F32)
        xi = jnp.zeros((size, 128), F32)
        for c in range(4):
            ir = im[0][:, 128 * c:128 * c + 128]
            ii = im[1][:, 128 * c:128 * c + 128]
            sr = s_vm[0, c, rows, :]
            si = s_vm[1, c, rows, :]
            xr = xr + (sr * ir + si * ii)
            xi = xi + (sr * ii - si * ir)
        return xr, xi

    y_copies = []
    for k in range(2):
        xr, xi = image_rows((1 - y_id) * 256 + 128 * k, 128)
        part[0, 128 * k:128 * k + 128] = xr
        part[1, 128 * k:128 * k + 128] = xi
        cp = remote(part.at[:, pl.ds(128 * k, 128)], rx2.at[:, pl.ds(128 * k, 128)], ysend.at[k], yrecv.at[k], mate)
        cp.start()
        y_copies.append(cp)
    for k in range(2):
        xr, xi = image_rows(y_id * 256 + 128 * k, 128)
        out_ref[0, 128 * k:128 * k + 128] = xr
        out_ref[1, 128 * k:128 * k + 128] = xi
    for k in range(2):
        y_copies[k].wait()
        sl = slice(128 * k, 128 * k + 128)
        out_ref[:, sl] += rx2[:, sl]


def combine(h_own, h_nb, e_own, e_nb, tab, maps):
    vm = pl.BlockSpec(memory_space=pltpu.VMEM)
    anym = pl.BlockSpec(memory_space=pl.ANY)
    dma = pltpu.SemaphoreType.DMA
    return pl.pallas_call(
        combine_kernel,
        out_shape=jax.ShapeDtypeStruct((2, 256, 128), F32),
        in_specs=[anym, anym, vm, vm, anym, anym],
        out_specs=vm,
        scratch_shapes=[
            pltpu.VMEM((2, 512, 2048), BF),
            pltpu.VMEM((2, 4, 256, 512), BF),
            pltpu.VMEM((2, 2, 2, 16, 512), BF),
            pltpu.VMEM((2, 4, 512, 128), F32),
            pltpu.VMEM((2, 2, 2, 16, 1024), F32),
            pltpu.VMEM((64, 2048), BF),
            pltpu.VMEM((4, 64, 128), F32),
            pltpu.VMEM((16, 512), F32),
            pltpu.VMEM((2, 256, 128), F32),
            pltpu.VMEM((2, 256, 128), F32),
            dma((16,)), dma((4,)), dma((2, 2)), dma((2, 2)), dma((2, 2)), dma((8,)), dma((8,)), dma((2,)), dma((2,)),
        ],
        compiler_params=pltpu.CompilerParams(vmem_limit_bytes=40 * 2**20, collective_id=0, has_side_effects=True),
        cost_estimate=pl.CostEstimate(flops=3 * 10**9, bytes_accessed=12 * 2**20, transcendentals=0),
        name='combine',
    )(h_own, h_nb, e_own, e_nb, tab, maps)


def solution(mesh):
    n_rows = mesh.shape['rows']
    swap = [(i, (i + 2) % n_rows) for i in range(n_rows)]

    def local_part(kspace, weight_row, weight_col, grid_row, grid_col, valid_count, coil_maps, deapod):
        n_img = deapod.shape[0]
        samples = kspace.shape[2]
        row_id = lax.axis_index('rows')
        coil_id = lax.axis_index('coil')
        local_row = (grid_row - row_id * (2 * n_img // n_rows)).astype(F32)
        packed = jnp.concatenate([
            kspace.reshape(8, samples), weight_row, weight_col, local_row[None], grid_col.astype(F32)[None],
            jnp.broadcast_to(valid_count.astype(F32)[:, None], (2, samples))], axis=0)
        other = lax.ppermute(packed, 'rows', swap)
        tab = jnp.asarray(tables(n_img))
        h_own, e_own = spread(packed, tab)
        h_nb, e_nb = spread(other, tab)
        combined = combine(h_own, h_nb, e_own, e_nb, tab, coil_maps)
        row_scale = lax.dynamic_slice_in_dim(deapod, coil_id * combined.shape[1], combined.shape[1])
        col_scale = lax.dynamic_slice_in_dim(deapod, row_id * combined.shape[2], combined.shape[2])
        return combined * (row_scale[:, None] * col_scale[None, :])[None]

    spec_samples = P(None, 'coil', ('slab', 'rows'))
    spec_weights = P(None, ('slab', 'rows'))
    spec_index = P(('slab', 'rows'))
    return jax.shard_map(local_part, mesh=mesh, in_specs=(spec_samples, spec_weights, spec_weights, spec_index, spec_index, spec_index, P(None, 'coil', 'slab', 'rows'), P()), out_specs=P(None, ('slab', 'coil'), 'rows'), check_vma=False)
```

time: 191 us -> 51.3 us (0.27)
  other arithmetic: 95 us -> 2.23 us
  Pallas kernels: 0 us -> 39.3 us
  matrix products: 30.5 us -> 0 us
  blocking collectives: 29.2 us -> 0 us
  between operations: 14.3 us -> 0.76 us
  waiting for transfers between devices: 12.6 us -> 0.01 us
    reduce_sum x3 -> x0, other arithmetic: 73.9 us -> none  [the longest x1 61.6 us: spread_block(): jnp.sum(jnp.where(row_offset[None, None, None] == kernel_idx[None, None,...]
    pallas_call x0 -> x3, Pallas kernels: none -> 39.3 us  [the longest x2 25 us: spread(): pl.pallas_call(spread_kernel, out_shape=(jax.ShapeDtypeStruct((2, 2, 256,...]
    dot_general x3 -> x0, matrix products: 30.5 us -> none  [the longest x1 20.6 us: spread_block(): jnp.einsum('qcrm,mk->qcrk', left_side, right_side, preferred_element_type...]
    all_to_all x1 -> x0, blocking collectives: 29.2 us -> none  [local_part(): columns = lax.all_to_all(half_image, 'rows', 3, 2, tiled=True)]
    reduce_scatter x1 -> x0, waiting for transfers between devices: 11.8 us -> none  [local_part(): lax.psum_scatter(jnp.stack([real_part, imag_part]), 'coil', scatter_dimen...]
    another operation x5 -> x0, other arithmetic: 10.5 us -> none
    select_n x1 -> x0, other arithmetic: 5.79 us -> none  [spread_block(): jnp.mod(jnp.arange(n_grid)[None, :] - grid_col[:, None] + half_width, n_g...]
    all_to_all x1 -> x0, local copies, waits for them, and re-layouts: 2.73 us -> none  [local_part(): columns = lax.all_to_all(half_image, 'rows', 3, 2, tiled=True)]
  transfers between devices with their start and end apart: 3 -> 1, of which waited for: 2 -> 0; matrix products, arithmetic and copies ran while one was open for 6% -> 0% of each run, Pallas kernels for 0% -> 18%
where the time goes in v1:
time: 51.3 us; the launch traced here: 51 us
  Pallas kernels  39.3 us (77%)
  local copies, waits for them, and re-layouts  5.29 us (10%)
  starting transfers between devices  3.36 us (7%)
  other arithmetic  2.23 us (4%)
  between operations  0.76 us (1%)
    pallas_call x2, Pallas kernels, spread(): pl.pallas_call(spread_kernel, out_shape=(jax.ShapeDtypeStruct((2, 2, 256,...  25 us
    pallas_call x1, Pallas kernels, combine(): pl.pallas_call(combine_kernel, out_shape=jax.ShapeDtypeStruct((2, 256, 12...  14.3 us
    ppermute x1, starting transfers between devices, local_part(): other = lax.ppermute(packed, 'rows', swap)  3.36 us
    unnamed x12, local copies, waits for them, and re-layouts  2.4 us
    concatenate x1, local copies, waits for them, and re-layouts, local_part(): jnp.concatenate([kspace.reshape(8, samples), weight_row, weight_col, loca...  1.87 us
  transfers between devices with their start and end apart: 1, of which 0 were waited for; matrix products, arithmetic and copies ran while one was open for 0% of the time, Pallas kernels for 18%

profile of v1, /device:TPU:0, one launch (start us, length us, event | category | flops | bytes accessed | tf_op | source)
XLA Modules:
  0.0 51.0 jit_solution(14138963191642741136)
XLA Ops:
  0.0 0.9 %reshape.31 = f32[8,2048]{1,0:T(8,128)S(1)} reshape(f32[2,4,2048]{2,1,0:T(4,128)} %param.9) | data formatting | bytes 131072 | tf_op jit(solution)/shard_map/reshape | solution.py:308
  0.9 0.7 %convert_element_type.10 = f32[2048]{0:T(1024)S(1)} convert(s32[2048]{0:T(1024)} %param.13) | non-fusion elementwise | flops 2048 | bytes 16384 | tf_op jit(solution)/shard_map/convert_element_type | solution.py:308
  2.2 0.7 %subtract_convert_fusion = f32[2048]{0:T(1024)S(1)} fusion(s32[2048]{0:T(1024)} %param.12, s32[]{:T(128)S(6)} %mul.34), kind=kLoop, calls=%fused_computation.2 | loop fusion | flops 4096 | bytes 16388 | tf_op jit(solution)/shard_map/convert_element_type | solution.py:306
  2.9 1.9 %concatenate.3.pk = f32[24,2048]{1,0:T(8,128)S(1)} concatenate(f32[8,2048]{1,0:T(8,128)S(1)} %reshape.31, f32[6,2048]{1,0:T(8,128)} %param.10, f32[6,2048]{1,0:T(8,128)} %param.11, f32[1,2048]{1,0:T(1,128)S(1)} %bitcast.4, f32[1,2048]{1,0:T(1,128)S(1)} %bitcast.3, f32[2,2048]{1,0:T(2,128)S(1)} %broadcast_in_dim.20), dimensions={0} | concatenate | bytes 393216 | tf_op jit(solution)/shard_map/concatenate | solution.py:307
  4.8 3.4 %collective-permute-start = (f32[24,2048]{1,0:T(8,128)S(1)}, f32[24,2048]{1,0:T(8,128)S(1)}, u32[]{:S(2)}, u32[]{:S(2)}) collective-permute-start(f32[24,2048]{1,0:T(8,128)S(1)} %concatenate.3.pk), channel_id=1, source_target_pairs={{0,2},{1,3},{2,0},{3,1},{4,6},{5,7},{6,4},{7,5}} | collective-permute-start | bytes 589832 | tf_op jit(solution)/shard_map/ppermute | solution.py:310
  8.2 0.0 copy-start.1
  8.2 1.6 %copy-done.1 = bf16[2,512,1024]{2,1,0:T(8,128)(2,1)S(1)} copy-done((bf16[2,512,1024]{2,1,0:T(8,128)(2,1)S(1)}, bf16[2,512,1024]{2,1,0:T(8,128)(2,1)}, u32[]{:S(2)}) %copy-start.1) | copy-done | bytes 2097176
  9.8 0.0 copy-start.5
  9.8 0.0 copy-start.2
  9.8 9.2 %spread.2 = (bf16[2,2,256,512]{3,2,1,0:T(8,128)(2,1)S(1)}, f32[2,64,1024]{2,1,0:T(8,128)S(1)}) custom-call(f32[24,2048]{1,0:T(8,128)S(1)} %concatenate.3.pk, bf16[2,512,1024]{2,1,0:T(8,128)(2,1)S(1)} %copy-done.1), custom_call_target="tpu_custom_call" | custom-call | flops 12999999488 | bytes 4194304 | tf_op jit(solution)/shard_map/spread/pallas_call | solution.py:118
  19.0 0.0 copy-start.3
  19.0 0.8 %copy-done.3 = f32[2,64,1024]{2,1,0:T(8,128)} copy-done((f32[2,64,1024]{2,1,0:T(8,128)}, f32[2,64,1024]{2,1,0:T(8,128)S(1)}, u32[]{:S(2)}) %copy-start.3) | copy-done | bytes 524312
  19.8 0.0 copy-done.5
  19.8 0.1 dynamic_slice.7
  19.9 0.1 dynamic_slice.6
  19.9 0.1 broadcast_multiply_fusion.1
  20.0 0.0 copy-start
  20.1 0.0 copy-start.4
  20.1 0.0 collective-permute-done.pk
  20.1 0.0 copy-done.2
  20.1 15.8 %spread.3 = (bf16[2,2,256,512]{3,2,1,0:T(8,128)(2,1)S(1)}, f32[2,64,1024]{2,1,0:T(8,128)S(1)}) custom-call(f32[24,2048]{1,0:T(8,128)S(1)} %collective-permute-done.pk, bf16[2,512,1024]{2,1,0:T(8,128)(2,1)S(1)} %copy-done.2), custom_call_target="tpu_custom_call" | custom-call | flops 12999999488 | bytes 4194304 | tf_op jit(solution)/shard_map/spread/pallas_call | solution.py:118
  35.9 0.0 copy-done
  35.9 0.0 copy-done.4
  36.0 14.3 %combine.1 = f32[2,256,128]{2,1,0:T(8,128)S(1)} custom-call(bf16[2,2,256,512]{3,2,1,0:T(8,128)(2,1)S(1)} %get-tuple-element.9.h_own, bf16[2,2,256,512]{3,2,1,0:T(8,128)(2,1)S(1)} %get-tuple-element.10.h_nb, f32[2,64,1024]{2,1,0:T(8,128)S(1)} %copy-done.4, f32[2,64,1024]{2,1,0:T(8,128)S(1)} %get-tuple-element.12.e_nb, bf16[2,512,1024]{2,1,0:T(8,128)(2,1)S(1)} %copy-done.2, ...), custom_call_target="tpu_custom_call" | custom-call | flops 3000000000 | bytes 12582912 | tf_op jit(solution)/shard_map/combine/pallas_call | solution.py:273
  50.2 0.7 %broadcast_multiply_fusion = f32[2,256,128]{2,1,0:T(8,128)} fusion(f32[2,256,128]{2,1,0:T(8,128)S(1)} %combine.1, f32[256,128]{1,0:T(8,128)S(1)} %broadcast_multiply_fusion.1), kind=kLoop, calls=%fused_computation | loop fusion | flops 65536 | bytes 655360 | tf_op jit(solution)/shard_map/mul | solution.py:317
  (1 shorter events, 0.0 us)
Async XLA Ops:
  4.8 15.3 %collective-permute-start = (f32[24,2048]{1,0:T(8,128)S(1)}, f32[24,2048]{1,0:T(8,128)S(1)}, u32[]{:S(2)}, u32[]{:S(2)}) collective-permute-start(f32[24,2048]{1,0:T(8,128)S(1)} %concatenate.3.pk), channel_id=1, source_target_pairs={{0,2},{1,3},{2,0},{3,1},{4,6},{5,7},{6,4},{7,5}} | collective-permute-start | bytes 589832 | tf_op jit(solution)/shard_map/ppermute | solution.py:310
  8.2 1.6 %copy-start.1 = (bf16[2,512,1024]{2,1,0:T(8,128)(2,1)S(1)}, bf16[2,512,1024]{2,1,0:T(8,128)(2,1)}, u32[]{:S(2)}) copy-start(bf16[2,512,1024]{2,1,0:T(8,128)(2,1)} %constant.19.clone.tab) | copy-start | bytes 6291460
  9.8 10.0 %copy-start.5 = (f32[512]{0:T(512)S(1)}, f32[512]{0:T(512)}, u32[]{:S(2)}) copy-start(f32[512]{0:T(512)} %param.16) | copy-start | bytes 6148
  9.8 10.3 %copy-start.2 = (bf16[2,512,1024]{2,1,0:T(8,128)(2,1)S(1)}, bf16[2,512,1024]{2,1,0:T(8,128)(2,1)}, u32[]{:S(2)}) copy-start(bf16[2,512,1024]{2,1,0:T(8,128)(2,1)} %constant.19.clone.tab) | copy-start | bytes 6291460
  19.0 0.8 %copy-start.3 = (f32[2,64,1024]{2,1,0:T(8,128)}, f32[2,64,1024]{2,1,0:T(8,128)S(1)}, u32[]{:S(2)}) copy-start(f32[2,64,1024]{2,1,0:T(8,128)S(1)} %get-tuple-element.11.e_own) | copy-start | bytes 1572868
  20.0 15.9 %copy-start = (f32[2,4,512,128]{3,2,1,0:T(8,128)S(1)}, f32[2,4,512,128]{3,2,1,0:T(8,128)}, u32[]{:S(2)}) copy-start(f32[2,4,512,128]{3,2,1,0:T(8,128)} %maps.1) | copy-start | bytes 6291460
  20.1 15.9 %copy-start.4 = (f32[2,64,1024]{2,1,0:T(8,128)S(1)}, f32[2,64,1024]{2,1,0:T(8,128)}, u32[]{:S(2)}) copy-start(f32[2,64,1024]{2,1,0:T(8,128)} %copy-done.3) | copy-start | bytes 1572868

commit v2 on v1

--- a/solution.py
+++ b/solution.py
@@ -22,7 +22,48 @@
     return np.stack([np.cos(ang), np.sin(ang)]).astype(np.float32).astype(BF)
 
 
-def spread_kernel(pk, tab, h_ref, e_ref, acc, a_buf, b_buf, g_buf, hs, t_buf, sem):
+def exchange_kernel(y_ref, wy_ref, wx_ref, iy_ref, ix_ref, n_ref, y_out, wy_out, wx_out, iy_out, ix_out, iy_in, loc, ssem, rsem):
+    row_id = lax.axis_index('rows')
+    other = {'rows': (row_id + 2) % 4}
+    iy_copy = pltpu.make_async_copy(iy_ref, iy_in, loc.at[4])
+    iy_copy.start()
+    pairs = [(y_ref, y_out), (wy_ref, wy_out), (wx_ref, wx_out), (ix_ref, ix_out)]
+    locs = [pltpu.make_async_copy(a, b.at[0], loc.at[i]) for i, (a, b) in enumerate(pairs)]
+    for cp in locs:
+        cp.start()
+    barrier = pltpu.get_barrier_semaphore()
+    pl.semaphore_signal(barrier, inc=1, device_id=other, device_id_type=pl.DeviceIdType.MESH)
+    iy_copy.wait()
+    slot = lax.broadcasted_iota(jnp.int32, iy_in.shape, 1)
+    iy_out[0] = jnp.where(slot < n_ref[0], iy_in[...] - row_id * 256, -1000)
+    pl.semaphore_wait(barrier, 1)
+    pairs.append((iy_out.at[0], iy_out))
+    sends = [pltpu.make_async_remote_copy(src_ref=a, dst_ref=b.at[1], send_sem=ssem.at[i], recv_sem=rsem.at[i], device_id=other, device_id_type=pl.DeviceIdType.MESH) for i, (a, b) in enumerate(pairs)]
+    for cp in sends:
+        cp.start()
+    for cp in locs:
+        cp.wait()
+    for cp in sends:
+        cp.wait()
+
+
+def exchange(y, wy, wx, iy, ix, n):
+    vm = pl.BlockSpec(memory_space=pltpu.VMEM)
+    anym = pl.BlockSpec(memory_space=pl.ANY)
+    dma = pltpu.SemaphoreType.DMA
+    return pl.pallas_call(
+        exchange_kernel,
+        out_shape=tuple(jax.ShapeDtypeStruct((2,) + v.shape, v.dtype) for v in (y, wy, wx, iy, ix)),
+        in_specs=[anym, anym, anym, anym, anym, pl.BlockSpec(memory_space=pltpu.SMEM)],
+        out_specs=(vm,) * 5,
+        scratch_shapes=[pltpu.VMEM(iy.shape, jnp.int32), dma((5,)), dma((5,)), dma((5,))],
+        compiler_params=pltpu.CompilerParams(vmem_limit_bytes=4 * 2**20, collective_id=1, has_side_effects=True),
+        cost_estimate=pl.CostEstimate(flops=10**9, bytes_accessed=10**6, transcendentals=0),
+        name='exchange',
+    )(y, wy, wx, iy, ix, n)
+
+
+def spread_kernel(y_ref, wy_ref, wx_ref, iy_ref, ix_ref, tab, h_ref, e_ref, acc, a_buf, b_buf, g_buf, hs, t_buf, sem):
     n_grid = 1024
     x_id = lax.axis_index('rows') // 2
     my_cols = pl.ds(pl.multiple_of(x_id * 256, 256), 256)
@@ -33,22 +74,19 @@
     ]
     for cp in copies:
         cp.start()
-    valid = jnp.max(pk[22:23, 0:128]).astype(jnp.int32)
-    n_chunk = (valid + (KC - 1)) // KC
-
-    def build(s):
+    def build(o, s):
         cols = pl.ds(pl.multiple_of(s * KC, KC), KC)
         sub = lax.broadcasted_iota(jnp.int32, (16, KC), 0)
-        keep = (lax.broadcasted_iota(jnp.int32, (1, KC), 1) + s * KC) < valid
-        r0 = pk[20:21, cols].astype(jnp.int32) + 1
+        r0 = iy_ref[o, :, cols] + 1
+        keep = r0 > 0
         u = jnp.broadcast_to((r0 >> 2).astype(F32), (16, KC)).astype(BF)
         t = (sub >> 2) - (r0 & 3)
         es = []
         for q in range(2):
             y16 = jnp.zeros((16, KC), F32)
             for c in range(4):
-                y16 = jnp.where((sub & 3) == c, pk[4 * q + c:4 * q + c + 1, cols], y16)
-            coef = [jnp.where(keep, y16 * pk[8 + a:9 + a, cols], 0.0) for a in range(6)]
+                y16 = jnp.where((sub & 3) == c, y_ref[o, q, c:c + 1, cols], y16)
+            coef = [jnp.where(keep, y16 * wy_ref[o, a:a + 1, cols], 0.0) for a in range(6)]
             row = []
             for j in range(3):
                 e = jnp.zeros((16, KC), F32)
@@ -64,14 +102,14 @@
             m2 = u == jnp.array(g - 2, BF)
             for q in range(2):
                 a_buf[1056 * q + 16 * g:1056 * q + 16 * g + 16, :] = jnp.where(m0, es[q][0], jnp.where(m1, es[q][1], jnp.where(m2, es[q][2], zero)))
-        c0 = (pk[21:22, cols].astype(jnp.int32) + (n_grid - 3)) & (n_grid - 1)
+        c0 = (ix_ref[o, :, cols] + (n_grid - 3)) & (n_grid - 1)
         uc = jnp.broadcast_to((c0 >> 4).astype(F32), (16, KC)).astype(BF)
         tc = sub - (c0 & 15)
         eb = []
         for j in range(2):
             e = jnp.zeros((16, KC), F32)
             for b in range(6):
-                e = jnp.where(tc == b - 16 * j, pk[14 + b:15 + b, cols], e)
+                e = jnp.where(tc == b - 16 * j, wx_ref[o, b:b + 1, cols], e)
             eb.append(e.astype(BF))
         for g in range(64):
             m0 = uc == jnp.array(g, BF)
@@ -88,37 +126,41 @@
             else:
                 acc[rows, :] += prod
 
-    build(0)
-    mults(True)
-
-    @pl.loop(1, n_chunk)
-    def _(s):
-        build(s)
-        mults(False)
-
     for cp in copies:
         cp.wait()
     t_buf[0, :, n_grid:] = -t_buf[1, :, :n_grid]
-    for q in range(2):
-        e_ref[q, 0:32] = acc[1056 * q:1056 * q + 32, :]
-        e_ref[q, 32:64] = acc[1056 * q + 1024:1056 * q + 1056, :]
-        g_buf[:, n_grid * q:n_grid * (q + 1)] = acc[1056 * q + 16:1056 * q + 1040, :].astype(BF)
-    for e in range(2):
-        prod = lax.dot_general(g_buf[...], t_buf[e], NT, preferred_element_type=F32)
-        for hc in range(2):
-            hs[2 * e + hc] = prod[:, 128 * hc:128 * hc + 128]
-    for e in range(2):
-        for hc in range(2):
-            for c in range(4):
-                h_ref[hc, e, :, 128 * c:128 * c + 128] = hs[2 * e + hc, pl.ds(c, 256, stride=4), :].astype(BF)
-
-
-def spread(pk, tab):
+
+    @pl.loop(0, 2)
+    def _(o):
+        valid = jnp.sum(jnp.where(iy_ref[o] >= 0, 1.0, 0.0)).astype(jnp.int32)
+        build(o, 0)
+        mults(True)
+
+        @pl.loop(1, (valid + (KC - 1)) // KC)
+        def _(s):
+            build(o, s)
+            mults(False)
+
+        for q in range(2):
+            e_ref[o, q, 0:32] = acc[1056 * q:1056 * q + 32, :]
+            e_ref[o, q, 32:64] = acc[1056 * q + 1024:1056 * q + 1056, :]
+            g_buf[:, n_grid * q:n_grid * (q + 1)] = acc[1056 * q + 16:1056 * q + 1040, :].astype(BF)
+        for e in range(2):
+            prod = lax.dot_general(g_buf[...], t_buf[e], NT, preferred_element_type=F32)
+            for hc in range(2):
+                hs[2 * e + hc] = prod[:, 128 * hc:128 * hc + 128]
+        for e in range(2):
+            for hc in range(2):
+                for c in range(4):
+                    h_ref[o, hc, e, :, 128 * c:128 * c + 128] = hs[2 * e + hc, pl.ds(c, 256, stride=4), :].astype(BF)
+
+
+def spread(y, wy, wx, iy, ix, tab):
     vm = pl.BlockSpec(memory_space=pltpu.VMEM)
     return pl.pallas_call(
         spread_kernel,
-        out_shape=(jax.ShapeDtypeStruct((2, 2, 256, 512), BF), jax.ShapeDtypeStruct((2, 64, 1024), F32)),
-        in_specs=[vm, pl.BlockSpec(memory_space=pl.ANY)],
+        out_shape=(jax.ShapeDtypeStruct((2, 2, 2, 256, 512), BF), jax.ShapeDtypeStruct((2, 2, 64, 1024), F32)),
+        in_specs=[vm, vm, vm, vm, vm, pl.BlockSpec(memory_space=pl.ANY)],
         out_specs=(vm, vm),
         scratch_shapes=[
             pltpu.VMEM((2112, 1024), F32),
@@ -132,11 +174,11 @@
         compiler_params=pltpu.CompilerParams(vmem_limit_bytes=40 * 2**20),
         cost_estimate=pl.CostEstimate(flops=13 * 10**9, bytes_accessed=4 * 2**20, transcendentals=0),
         name='spread',
-    )(pk, tab)
-
-
-def combine_kernel(h_own, h_nb, e_own, e_nb, tab, maps, out_ref,
-                   t3, rhs, sbuf, s_vm, rx, ge, hs, pt, part, rx2,
+    )(y, wy, wx, iy, ix, tab)
+
+
+def combine_kernel(hh, ee, tab, maps, dd, out_ref,
+                   t3, rhs, sbuf, s_vm, rx, ge, hs, pt, part, rx2, scale,
                    loc, esend, erecv, hsend, hrecv, psend, precv, ysend, yrecv):
     n_grid = 1024
     row_id = lax.axis_index('rows')
@@ -146,8 +188,6 @@
     sib = {'rows': row_id + 1 - 2 * core}
     mate = {'coil': 1 - y_id}
     blocks = [row_id, (row_id + 2) % 4]
-    hh = [h_own, h_nb]
-    ee = [e_own, e_nb]
 
     n_loc = 0
     t_copies = []
@@ -157,10 +197,10 @@
     h_copies = []
     for o in range(2):
         for b in range(2):
-            h_copies.append(pltpu.make_async_copy(hh[o].at[core, b], rhs.at[b, blocks[o]], loc.at[n_loc]))
+            h_copies.append(pltpu.make_async_copy(hh.at[o, core, b], rhs.at[b, blocks[o]], loc.at[n_loc]))
             n_loc += 1
             for end in range(2):
-                h_copies.append(pltpu.make_async_copy(hh[o].at[1 - core, b, pl.ds(240 * end, 16)], sbuf.at[o, b, end], loc.at[n_loc]))
+                h_copies.append(pltpu.make_async_copy(hh.at[o, 1 - core, b, pl.ds(240 * end, 16)], sbuf.at[o, b, end], loc.at[n_loc]))
                 n_loc += 1
     s_copy = pltpu.make_async_copy(maps, s_vm, loc.at[n_loc])
     for cp in t_copies + h_copies:
@@ -179,16 +219,18 @@
         low = o * core + (1 - o) * (1 - core)
         high = o * (1 - core) + (1 - o) * core
         for k, (slot, end, row0) in enumerate(((low, 1, 0), (high, 0, 48))):
-            e_copies.append(remote(ee[o].at[:, pl.ds(row0, 16)], rx.at[slot, end], esend.at[2 * o + k], erecv.at[slot, end], sib))
+            e_copies.append(remote(ee.at[o, :, pl.ds(row0, 16)], rx.at[slot, end], esend.at[2 * o + k], erecv.at[slot, end], sib))
     for cp in e_copies:
         cp.start()
     hr_copies = []
     for o in range(2):
         for b in range(2):
-            hr_copies.append(remote(hh[o].at[1 - core, b, pl.ds(16, 224)], rhs.at[b, blocks[o], pl.ds(16, 224)], hsend.at[o, b], hrecv.at[o, b], sib))
+            hr_copies.append(remote(hh.at[o, 1 - core, b, pl.ds(16, 224)], rhs.at[b, blocks[o], pl.ds(16, 224)], hsend.at[o, b], hrecv.at[o, b], sib))
     for cp in hr_copies:
         cp.start()
     s_copy.start()
+    row_scale = jnp.broadcast_to(dd[:, pl.ds(pl.multiple_of(y_id * 256, 256), 256)], (128, 256)).T
+    scale[...] = row_scale * dd[:, pl.ds(pl.multiple_of(row_id * 128, 128), 128)]
 
     for cp in t_copies:
         cp.wait()
@@ -199,7 +241,7 @@
         for end in range(2):
             remote(rx.at[o, end], rx.at[o, end], esend.at[2 * o + end], erecv.at[o, end], sib).wait_recv()
             for q in range(2):
-                ge[32 * o + 16 * end:32 * o + 16 * end + 16, n_grid * q:n_grid * (q + 1)] = (ee[o][q, 16 + 16 * end:32 + 16 * end, :] + rx[o, end, q]).astype(BF)
+                ge[32 * o + 16 * end:32 * o + 16 * end + 16, n_grid * q:n_grid * (q + 1)] = (ee[o, q, 16 + 16 * end:32 + 16 * end, :] + rx[o, end, q]).astype(BF)
     cols = pl.ds(pl.multiple_of(x_id * 256, 256), 256)
     for e in range(2):
         prod = lax.dot_general(ge[...], t3[e, cols, :], NT, preferred_element_type=F32)
@@ -263,17 +305,18 @@
     for k in range(2):
         y_copies[k].wait()
         sl = slice(128 * k, 128 * k + 128)
-        out_ref[:, sl] += rx2[:, sl]
-
-
-def combine(h_own, h_nb, e_own, e_nb, tab, maps):
+        for e in range(2):
+            out_ref[e, sl] = (out_ref[e, sl] + rx2[e, sl]) * scale[sl]
+
+
+def combine(hh, ee, tab, maps, dd):
     vm = pl.BlockSpec(memory_space=pltpu.VMEM)
     anym = pl.BlockSpec(memory_space=pl.ANY)
     dma = pltpu.SemaphoreType.DMA
     return pl.pallas_call(
         combine_kernel,
         out_shape=jax.ShapeDtypeStruct((2, 256, 128), F32),
-        in_specs=[anym, anym, vm, vm, anym, anym],
+        in_specs=[anym, vm, anym, anym, vm],
         out_specs=vm,
         scratch_shapes=[
             pltpu.VMEM((2, 512, 2048), BF),
@@ -286,35 +329,23 @@
             pltpu.VMEM((16, 512), F32),
             pltpu.VMEM((2, 256, 128), F32),
             pltpu.VMEM((2, 256, 128), F32),
+            pltpu.VMEM((256, 128), F32),
             dma((16,)), dma((4,)), dma((2, 2)), dma((2, 2)), dma((2, 2)), dma((8,)), dma((8,)), dma((2,)), dma((2,)),
         ],
         compiler_params=pltpu.CompilerParams(vmem_limit_bytes=40 * 2**20, collective_id=0, has_side_effects=True),
         cost_estimate=pl.CostEstimate(flops=3 * 10**9, bytes_accessed=12 * 2**20, transcendentals=0),
         name='combine',
-    )(h_own, h_nb, e_own, e_nb, tab, maps)
+    )(hh, ee, tab, maps, dd)
 
 
 def solution(mesh):
-    n_rows = mesh.shape['rows']
-    swap = [(i, (i + 2) % n_rows) for i in range(n_rows)]
-
     def local_part(kspace, weight_row, weight_col, grid_row, grid_col, valid_count, coil_maps, deapod):
         n_img = deapod.shape[0]
-        samples = kspace.shape[2]
-        row_id = lax.axis_index('rows')
-        coil_id = lax.axis_index('coil')
-        local_row = (grid_row - row_id * (2 * n_img // n_rows)).astype(F32)
-        packed = jnp.concatenate([
-            kspace.reshape(8, samples), weight_row, weight_col, local_row[None], grid_col.astype(F32)[None],
-            jnp.broadcast_to(valid_count.astype(F32)[:, None], (2, samples))], axis=0)
-        other = lax.ppermute(packed, 'rows', swap)
+        hbm = [pltpu.with_memory_space_constraint(v, pltpu.HBM) for v in (kspace, weight_row, weight_col, grid_row[None], grid_col[None])]
+        stacked = exchange(*hbm, valid_count)
         tab = jnp.asarray(tables(n_img))
-        h_own, e_own = spread(packed, tab)
-        h_nb, e_nb = spread(other, tab)
-        combined = combine(h_own, h_nb, e_own, e_nb, tab, coil_maps)
-        row_scale = lax.dynamic_slice_in_dim(deapod, coil_id * combined.shape[1], combined.shape[1])
-        col_scale = lax.dynamic_slice_in_dim(deapod, row_id * combined.shape[2], combined.shape[2])
-        return combined * (row_scale[:, None] * col_scale[None, :])[None]
+        hh, ee = spread(*stacked, tab)
+        return combine(hh, ee, tab, coil_maps, deapod[None])
 
     spec_samples = P(None, 'coil', ('slab', 'rows'))
     spec_weights = P(None, ('slab', 'rows'))

time: 51.3 us -> 49.4 us (0.963); the launches traced: 51 us -> 49.8 us
  Pallas kernels: 39.3 us -> 48.2 us
  local copies, waits for them, and re-layouts: 5.29 us -> 0.72 us
  starting transfers between devices: 3.36 us -> 0 us
  other arithmetic: 2.23 us -> 0 us
    pallas_call x2, Pallas kernels: 25 us -> 34.1 us  [the longest x1 24.7 us: spread(): pl.pallas_call(spread_kernel, out_shape=(jax.ShapeDtypeStruct((2, 2, 2, 2...]
    ppermute x1 -> x0, starting transfers between devices: 3.36 us -> none  [local_part(): other = lax.ppermute(packed, 'rows', swap)]
    concatenate x1 -> x0, local copies, waits for them, and re-layouts: 1.87 us -> none  [local_part(): jnp.concatenate([kspace.reshape(8, samples), weight_row, weight_col, loca...]
    unnamed x12 -> x7, local copies, waits for them, and re-layouts: 2.4 us -> 0.72 us
    convert_element_type x2 -> x0, other arithmetic: 1.4 us -> none  [the longest x1 0.7 us: local_part(): local_row = (grid_row - row_id * (2 * n_img // n_rows)).astype(F32)]
    reshape x1 -> x0, local copies, waits for them, and re-layouts: 0.86 us -> none  [local_part(): kspace.reshape(8, samples)]
    mul x2 -> x0, other arithmetic: 0.82 us -> none  [local_part(): return combined * (row_scale[:, None] * col_scale[None, :])[None]]
  transfers between devices with their start and end apart: 1 -> 0, of which waited for: 0 -> 0; matrix products, arithmetic and copies ran while one was open for 0% -> 0% of each run, Pallas kernels for 18% -> 0%
where the time goes in v2:
time: 49.4 us; the launch traced here: 49.8 us
  Pallas kernels  48.2 us (98%)
  between operations  0.87 us (2%)
  local copies, waits for them, and re-layouts  0.72 us (1%)
    pallas_call x1, Pallas kernels, spread(): pl.pallas_call(spread_kernel, out_shape=(jax.ShapeDtypeStruct((2, 2, 2, 2...  24.7 us
    pallas_call x1, Pallas kernels, combine(): pl.pallas_call(combine_kernel, out_shape=jax.ShapeDtypeStruct((2, 256, 12...  14.1 us
    pallas_call x1, Pallas kernels, exchange(): pl.pallas_call(exchange_kernel, out_shape=tuple((jax.ShapeDtypeStruct((2,...  9.44 us

profile of v2, /device:TPU:0, one launch (start us, length us, event | category | flops | bytes accessed | tf_op | source)
XLA Modules:
  0.0 49.8 jit_solution(3787802307414460581)
XLA Ops:
  0.0 0.0 copy-start.2
  0.8 9.4 %exchange.1 = (f32[2,2,4,2048]{3,2,1,0:T(4,128)S(1)}, f32[2,6,2048]{2,1,0:T(8,128)S(1)}, f32[2,6,2048]{2,1,0:T(8,128)S(1)}, s32[2,1,2048]{2,1,0:T(1,128)S(1)}, s32[2,1,2048]{2,1,0:T(1,128)S(1)}) custom-call(f32[2,4,2048]{2,1,0:T(4,128)} %y_ref.1, f32[6,2048]{1,0:T(8,128)} %wy_ref.1, f32[6,2048]{1,0:T(8,128)} %wx_ref.1, s32[1,2048]{1,0:T(1,128)} %bitcast.4, ...), custom_call_target="tpu_custom_call" | custom-call | flops 1000000000 | bytes 1000000 | tf_op jit(solution)/shard_map/exchange/pallas_call | solution.py:54
  10.3 0.0 copy-done.2
  10.3 0.0 copy-start
  10.3 0.0 copy-start.1
  10.3 24.7 %spread.1 = (bf16[2,2,2,256,512]{4,3,2,1,0:T(8,128)(2,1)S(1)}, f32[2,2,64,1024]{3,2,1,0:T(8,128)S(1)}) custom-call(f32[2,2,4,2048]{3,2,1,0:T(4,128)S(1)} %get-tuple-element.12.y_ref, f32[2,6,2048]{2,1,0:T(8,128)S(1)} %get-tuple-element.13.wy_ref, f32[2,6,2048]{2,1,0:T(8,128)S(1)} %get-tuple-element.14.wx_ref, s32[2,1,2048]{2,1,0:T(1,128)S(1)} %get-tuple-element.15.iy_ref, ...), custom_call_target="tpu_custom_call" | custom-call | flops 12999999488 | bytes 4194304 | tf_op jit(solution)/shard_map/spread/pallas_call | solution.py:160
  35.0 0.0 copy-done
  35.0 0.0 copy-done.1
  35.0 14.1 %combine.1 = f32[2,256,128]{2,1,0:T(8,128)S(1)} custom-call(bf16[2,2,2,256,512]{4,3,2,1,0:T(8,128)(2,1)S(1)} %get-tuple-element.17.hh, f32[2,2,64,1024]{3,2,1,0:T(8,128)S(1)} %get-tuple-element.18.ee, bf16[2,512,1024]{2,1,0:T(8,128)(2,1)S(1)} %copy-done.2, f32[2,4,512,128]{3,2,1,0:T(8,128)S(1)} %copy-done, f32[1,512]{1,0:T(1,128)S(1)} %bitcast.3), custom_call_target="tpu_custom_call" | custom-call | flops 3000000000 | bytes 12582912 | tf_op jit(solution)/shard_map/combine/pallas_call | solution.py:316
  49.1 0.7 %copy.12 = f32[2,256,128]{2,1,0:T(8,128)} copy(f32[2,256,128]{2,1,0:T(8,128)S(1)} %combine.1) | data formatting | bytes 524288
Async XLA Ops:
  0.0 10.3 %copy-start.2 = (bf16[2,512,1024]{2,1,0:T(8,128)(2,1)S(1)}, bf16[2,512,1024]{2,1,0:T(8,128)(2,1)}, u32[]{:S(2)}) copy-start(bf16[2,512,1024]{2,1,0:T(8,128)(2,1)} %constant.2.clone.tab) | copy-start | bytes 6291460
  10.3 24.7 %copy-start = (f32[2,4,512,128]{3,2,1,0:T(8,128)S(1)}, f32[2,4,512,128]{3,2,1,0:T(8,128)}, u32[]{:S(2)}) copy-start(f32[2,4,512,128]{3,2,1,0:T(8,128)} %maps.1) | copy-start | bytes 6291460
  10.3 24.7 %copy-start.1 = (f32[512]{0:T(512)S(1)}, f32[512]{0:T(512)}, u32[]{:S(2)}) copy-start(f32[512]{0:T(512)} %param.16) | copy-start | bytes 6148

commit v3 on v2

--- a/solution.py
+++ b/solution.py
@@ -12,6 +12,10 @@
 BF = jnp.bfloat16
 NT = (((1,), (1,)), ((), ()))
 KC = 512
+GRID = 1024
+SAMPLES = 2048
+RUN = 256
+WIN = 12
 
 
 def tables(n_img):
@@ -22,129 +26,174 @@
     return np.stack([np.cos(ang), np.sin(ang)]).astype(np.float32).astype(BF)
 
 
-def exchange_kernel(y_ref, wy_ref, wx_ref, iy_ref, ix_ref, n_ref, y_out, wy_out, wx_out, iy_out, ix_out, iy_in, loc, ssem, rsem):
-    row_id = lax.axis_index('rows')
-    other = {'rows': (row_id + 2) % 4}
-    iy_copy = pltpu.make_async_copy(iy_ref, iy_in, loc.at[4])
-    iy_copy.start()
-    pairs = [(y_ref, y_out), (wy_ref, wy_out), (wx_ref, wx_out), (ix_ref, ix_out)]
-    locs = [pltpu.make_async_copy(a, b.at[0], loc.at[i]) for i, (a, b) in enumerate(pairs)]
-    for cp in locs:
-        cp.start()
-    barrier = pltpu.get_barrier_semaphore()
-    pl.semaphore_signal(barrier, inc=1, device_id=other, device_id_type=pl.DeviceIdType.MESH)
-    iy_copy.wait()
-    slot = lax.broadcasted_iota(jnp.int32, iy_in.shape, 1)
-    iy_out[0] = jnp.where(slot < n_ref[0], iy_in[...] - row_id * 256, -1000)
-    pl.semaphore_wait(barrier, 1)
-    pairs.append((iy_out.at[0], iy_out))
-    sends = [pltpu.make_async_remote_copy(src_ref=a, dst_ref=b.at[1], send_sem=ssem.at[i], recv_sem=rsem.at[i], device_id=other, device_id_type=pl.DeviceIdType.MESH) for i, (a, b) in enumerate(pairs)]
-    for cp in sends:
-        cp.start()
-    for cp in locs:
-        cp.wait()
-    for cp in sends:
-        cp.wait()
-
-
-def exchange(y, wy, wx, iy, ix, n):
-    vm = pl.BlockSpec(memory_space=pltpu.VMEM)
-    anym = pl.BlockSpec(memory_space=pl.ANY)
-    dma = pltpu.SemaphoreType.DMA
-    return pl.pallas_call(
-        exchange_kernel,
-        out_shape=tuple(jax.ShapeDtypeStruct((2,) + v.shape, v.dtype) for v in (y, wy, wx, iy, ix)),
-        in_specs=[anym, anym, anym, anym, anym, pl.BlockSpec(memory_space=pltpu.SMEM)],
-        out_specs=(vm,) * 5,
-        scratch_shapes=[pltpu.VMEM(iy.shape, jnp.int32), dma((5,)), dma((5,)), dma((5,))],
-        compiler_params=pltpu.CompilerParams(vmem_limit_bytes=4 * 2**20, collective_id=1, has_side_effects=True),
-        cost_estimate=pl.CostEstimate(flops=10**9, bytes_accessed=10**6, transcendentals=0),
-        name='exchange',
-    )(y, wy, wx, iy, ix, n)
-
-
-def spread_kernel(y_ref, wy_ref, wx_ref, iy_ref, ix_ref, tab, h_ref, e_ref, acc, a_buf, b_buf, g_buf, hs, t_buf, sem):
-    n_grid = 1024
-    x_id = lax.axis_index('rows') // 2
-    my_cols = pl.ds(pl.multiple_of(x_id * 256, 256), 256)
-    copies = [
-        pltpu.make_async_copy(tab.at[0, my_cols], t_buf.at[0, :, pl.ds(0, n_grid)], sem.at[0]),
-        pltpu.make_async_copy(tab.at[1, my_cols], t_buf.at[1, :, pl.ds(0, n_grid)], sem.at[1]),
-        pltpu.make_async_copy(tab.at[0, my_cols], t_buf.at[1, :, pl.ds(n_grid, n_grid)], sem.at[2]),
-    ]
-    for cp in copies:
-        cp.start()
-    def build(o, s):
+def payload(y_ref, wy_ref, wx_ref, iy_ref, ix_ref, pay):
+    @pl.loop(0, SAMPLES // KC)
+    def _(s):
         cols = pl.ds(pl.multiple_of(s * KC, KC), KC)
         sub = lax.broadcasted_iota(jnp.int32, (16, KC), 0)
-        r0 = iy_ref[o, :, cols] + 1
-        keep = r0 > 0
-        u = jnp.broadcast_to((r0 >> 2).astype(F32), (16, KC)).astype(BF)
-        t = (sub >> 2) - (r0 & 3)
-        es = []
+        r0 = iy_ref[:, cols] + 1
+        counted = r0 > 0
+        t = jnp.where(counted, (sub >> 2) - (r0 & 3), 100)
         for q in range(2):
             y16 = jnp.zeros((16, KC), F32)
             for c in range(4):
-                y16 = jnp.where((sub & 3) == c, y_ref[o, q, c:c + 1, cols], y16)
-            coef = [jnp.where(keep, y16 * wy_ref[o, a:a + 1, cols], 0.0) for a in range(6)]
-            row = []
+                y16 = jnp.where((sub & 3) == c, y_ref[q, c:c + 1, cols], y16)
+            coef = [y16 * wy_ref[a:a + 1, cols] for a in range(6)]
             for j in range(3):
                 e = jnp.zeros((16, KC), F32)
                 for a in range(6):
                     if -3 <= a - 4 * j <= 3:
                         e = jnp.where(t == a - 4 * j, coef[a], e)
-                row.append(e.astype(BF))
-            es.append(row)
-        zero = jnp.zeros((16, KC), BF)
-        for g in range(66):
-            m0 = u == jnp.array(g, BF)
-            m1 = u == jnp.array(g - 1, BF)
-            m2 = u == jnp.array(g - 2, BF)
-            for q in range(2):
-                a_buf[1056 * q + 16 * g:1056 * q + 16 * g + 16, :] = jnp.where(m0, es[q][0], jnp.where(m1, es[q][1], jnp.where(m2, es[q][2], zero)))
-        c0 = (ix_ref[o, :, cols] + (n_grid - 3)) & (n_grid - 1)
-        uc = jnp.broadcast_to((c0 >> 4).astype(F32), (16, KC)).astype(BF)
-        tc = sub - (c0 & 15)
-        eb = []
+                pay[48 * q + 16 * j:48 * q + 16 * j + 16, cols] = e.astype(BF)
+        c0 = (ix_ref[:, cols] + (GRID - 3)) & (GRID - 1)
+        tc = jnp.where(counted, sub - (c0 & 15), 100)
         for j in range(2):
             e = jnp.zeros((16, KC), F32)
             for b in range(6):
-                e = jnp.where(tc == b - 16 * j, wx_ref[o, b:b + 1, cols], e)
-            eb.append(e.astype(BF))
+                e = jnp.where(tc == b - 16 * j, wx_ref[b:b + 1, cols], e)
+            pay[96 + 16 * j:112 + 16 * j, cols] = e.astype(BF)
+        pay[128:144, cols] = jnp.broadcast_to(((r0 >> 2) + 1).astype(F32), (16, KC)).astype(BF)
+        pay[144:160, cols] = jnp.broadcast_to((c0 >> 4).astype(F32), (16, KC)).astype(BF)
+
+
+def iota16():
+    return lax.broadcasted_iota(jnp.int32, (16, 1), 0).astype(F32)
+
+
+def ranks(iy_ref, oh, rank):
+    n_run = SAMPLES // RUN
+    for ch in range(n_run):
+        lanes = slice(RUN * ch, RUN * ch + RUN)
+        bucket = jnp.broadcast_to(((iy_ref[:, lanes] + 1) >> 2).astype(F32), (16, RUN)).astype(BF)
+        for g in range(5):
+            oh[80 * ch + 16 * g:80 * ch + 16 * g + 16, :] = jnp.where(bucket == (iota16() + 16 * g).astype(BF), jnp.ones((), BF), jnp.zeros((), BF))
+    lower = lax.broadcasted_iota(jnp.int32, (RUN, RUN + 128), 0)
+    upper = lax.broadcasted_iota(jnp.int32, (RUN, RUN + 128), 1)
+    tri = jnp.where((lower < upper) | (upper >= RUN), 1.0, 0.0).astype(BF)
+    pre = jnp.dot(oh[...], tri, preferred_element_type=F32)
+    counts = [pre[80 * ch:80 * ch + 80, RUN:] for ch in range(n_run)]
+    total = counts[0]
+    for ch in range(1, n_run):
+        total = total + counts[ch]
+    high = jnp.floor(total * (1.0 / 256.0))
+    low = total - 256.0 * high
+    strict = jnp.where(lax.broadcasted_iota(jnp.int32, (80, 80), 1) < lax.broadcasted_iota(jnp.int32, (80, 80), 0), 1.0, 0.0).astype(BF)
+    base = 256.0 * jnp.dot(strict, high.astype(BF), preferred_element_type=F32) + jnp.dot(strict, low.astype(BF), preferred_element_type=F32)
+    for ch in range(n_run):
+        lanes = slice(RUN * ch, RUN * ch + RUN)
+        place = pre[80 * ch:80 * ch + 80, :RUN] + jnp.concatenate([base] * (RUN // 128), axis=1)
+        place = jnp.sum(oh[80 * ch:80 * ch + 80, :].astype(F32) * place, axis=0, keepdims=True)
+        rank[:, lanes] = jnp.where(iy_ref[:, lanes] >= 0, place, -1.0)
+        base = base + counts[ch]
+
+
+def reorder(s, pay, rank, pt):
+    place = jnp.broadcast_to(rank[...] - (s * RUN).astype(F32), (16, SAMPLES)).astype(BF)
+    for g in range(RUN // 16):
+        pt[16 * g:16 * g + 16, :] = jnp.where(place == (iota16() + 16 * g).astype(BF), jnp.ones((), BF), jnp.zeros((), BF))
+    return lax.dot_general(pay[...], pt[...], NT, preferred_element_type=F32).astype(BF)
+
+
+def exchange_kernel(y_ref, wy_ref, wx_ref, iy_ref, ix_ref, n_ref, y_out, wy_out, wx_out, iy_out, ix_out, d_out,
+                    y_in, wy_in, wx_in, iy_in, ix_in, iy_raw, pay, oh, rank, pt, loc, ssem, rsem):
+    row_id = lax.axis_index('rows')
+    other = {'rows': (row_id + 2) % 4}
+    iy_copy = pltpu.make_async_copy(iy_ref, iy_raw, loc.at[4])
+    iy_copy.start()
+    trips = [(y_ref, y_in, y_out), (wy_ref, wy_in, wy_out), (wx_ref, wx_in, wx_out), (ix_ref, ix_in, ix_out)]
+    locs = [pltpu.make_async_copy(a, b, loc.at[i]) for i, (a, b, _) in enumerate(trips)]
+    for cp in locs:
+        cp.start()
+    barrier = pltpu.get_barrier_semaphore()
+    pl.semaphore_signal(barrier, inc=1, device_id=other, device_id_type=pl.DeviceIdType.MESH)
+    iy_copy.wait()
+    slot = lax.broadcasted_iota(jnp.int32, iy_in.shape, 1)
+    iy_in[...] = jnp.where(slot < n_ref[0], iy_raw[...] - row_id * 256, -1000)
+    pl.semaphore_wait(barrier, 1)
+    trips.append((iy_in, None, iy_out))
+    sends = [pltpu.make_async_remote_copy(src_ref=a, dst_ref=b, send_sem=ssem.at[i], recv_sem=rsem.at[i], device_id=other, device_id_type=pl.DeviceIdType.MESH) for i, (a, _, b) in enumerate(trips)]
+    for cp in sends:
+        cp.start()
+    for cp in locs:
+        cp.wait()
+    payload(y_in, wy_in, wx_in, iy_in, ix_in, pay)
+    ranks(iy_in, oh, rank)
+
+    @pl.loop(0, SAMPLES // RUN)
+    def _(s):
+        d_out[s] = reorder(s, pay, rank, pt)
+
+    for cp in sends:
+        cp.wait()
+
+
+def sort_scratch():
+    return [pltpu.VMEM((160, SAMPLES), BF), pltpu.VMEM((80 * (SAMPLES // RUN), RUN), BF), pltpu.VMEM((1, SAMPLES), F32), pltpu.VMEM((RUN, SAMPLES), BF)]
+
+
+def exchange(y, wy, wx, iy, ix, n):
+    vm = pl.BlockSpec(memory_space=pltpu.VMEM)
+    anym = pl.BlockSpec(memory_space=pl.ANY)
+    dma = pltpu.SemaphoreType.DMA
+    raw = (y, wy, wx, iy, ix)
+    return pl.pallas_call(
+        exchange_kernel,
+        out_shape=tuple(jax.ShapeDtypeStruct(v.shape, v.dtype) for v in raw) + (jax.ShapeDtypeStruct((SAMPLES // RUN, 160, RUN), BF),),
+        in_specs=[anym, anym, anym, anym, anym, pl.BlockSpec(memory_space=pltpu.SMEM)],
+        out_specs=(vm,) * 6,
+        scratch_shapes=[pltpu.VMEM(v.shape, v.dtype) for v in raw + (iy,)] + sort_scratch() + [dma((5,)), dma((5,)), dma((5,))],
+        compiler_params=pltpu.CompilerParams(vmem_limit_bytes=12 * 2**20, collective_id=1, has_side_effects=True),
+        cost_estimate=pl.CostEstimate(flops=10**9, bytes_accessed=10**6, transcendentals=0),
+        name='exchange',
+    )(y, wy, wx, iy, ix, n)
+
+
+def spread_kernel(y_ref, wy_ref, wx_ref, iy_ref, ix_ref, d_own, tab, h_ref, e_ref,
+                  n_buf, d_nb, pay, oh, rank, pt, acc, a_buf, b_buf, g_buf, hs, t_buf, sem):
+    x_id = lax.axis_index('rows') // 2
+    my_cols = pl.ds(pl.multiple_of(x_id * 256, 256), 256)
+    copies = [
+        pltpu.make_async_copy(tab.at[0, my_cols], t_buf.at[0, :, pl.ds(0, GRID)], sem.at[0]),
+        pltpu.make_async_copy(tab.at[1, my_cols], t_buf.at[1, :, pl.ds(0, GRID)], sem.at[1]),
+        pltpu.make_async_copy(tab.at[0, my_cols], t_buf.at[1, :, pl.ds(GRID, GRID)], sem.at[2]),
+    ]
+    for cp in copies:
+        cp.start()
+    zero = jnp.zeros((16, RUN), BF)
+
+    def run(d_ref, s):
+        first = jnp.sum(jnp.where(lax.broadcasted_iota(jnp.int32, (1, RUN), 1) == 0, d_ref[s, 128:129, :].astype(F32), 0.0)).astype(jnp.int32) - 1
+        last = jnp.max(d_ref[s, 128:129, :].astype(F32)).astype(jnp.int32) + 1
+        uc = d_ref[s, 144:160, :]
+        eb = [d_ref[s, 96 + 16 * j:112 + 16 * j, :] for j in range(2)]
         for g in range(64):
-            m0 = uc == jnp.array(g, BF)
-            m1 = uc == jnp.array((g - 1) % 64, BF)
-            b_buf[16 * g:16 * g + 16, :] = jnp.where(m0, eb[0], jnp.where(m1, eb[1], zero))
-
-    def mults(first):
-        @pl.loop(0, 2)
-        def _(q):
-            rows = pl.ds(pl.multiple_of(q * 1056, 16), 1056)
-            prod = lax.dot_general(a_buf[rows, :], b_buf[...], NT, preferred_element_type=F32)
-            if first:
-                acc[rows, :] = prod
-            else:
-                acc[rows, :] += prod
-
-    for cp in copies:
-        cp.wait()
-    t_buf[0, :, n_grid:] = -t_buf[1, :, :n_grid]
-
-    @pl.loop(0, 2)
-    def _(o):
-        valid = jnp.sum(jnp.where(iy_ref[o] >= 0, 1.0, 0.0)).astype(jnp.int32)
-        build(o, 0)
-        mults(True)
-
-        @pl.loop(1, (valid + (KC - 1)) // KC)
+            b_buf[16 * g:16 * g + 16, :] = jnp.where(uc == jnp.array(g, BF), eb[0], jnp.where(uc == jnp.array((g - 1) % 64, BF), eb[1], zero))
+
+        @pl.loop(0, (last - first + WIN) // WIN)
+        def _(w):
+            g0 = first + WIN * w
+            rel = (d_ref[s, 128:144, :].astype(F32) - (g0 + 1).astype(F32)).astype(BF)
+            for gi in range(WIN):
+                m = [rel == jnp.array(gi - j, BF) for j in range(3)]
+                for q in range(2):
+                    e = [d_ref[s, 48 * q + 16 * j:48 * q + 16 * j + 16, :] for j in range(3)]
+                    a_buf[16 * (WIN * q + gi):16 * (WIN * q + gi) + 16, :] = jnp.where(m[0], e[0], jnp.where(m[1], e[1], jnp.where(m[2], e[2], zero)))
+            prod = lax.dot_general(a_buf[...], b_buf[...], NT, preferred_element_type=F32)
+            rows = pl.ds(pl.multiple_of(g0 * 16, 16), 16 * WIN)
+            for q in range(2):
+                acc[q, rows, :] += prod[16 * WIN * q:16 * WIN * (q + 1)]
+
+    def block(o, d_ref, n_runs):
+        acc[...] = jnp.zeros_like(acc)
+
+        @pl.loop(0, n_runs)
         def _(s):
-            build(o, s)
-            mults(False)
+            run(d_ref, s)
 
         for q in range(2):
-            e_ref[o, q, 0:32] = acc[1056 * q:1056 * q + 32, :]
-            e_ref[o, q, 32:64] = acc[1056 * q + 1024:1056 * q + 1056, :]
-            g_buf[:, n_grid * q:n_grid * (q + 1)] = acc[1056 * q + 16:1056 * q + 1040, :].astype(BF)
+            e_ref[o, q, 0:32] = acc[q, 0:32, :]
+            e_ref[o, q, 32:64] = acc[q, 1024:1056, :]
+            g_buf[:, GRID * q:GRID * (q + 1)] = acc[q, 16:1040, :].astype(BF)
         for e in range(2):
             prod = lax.dot_general(g_buf[...], t_buf[e], NT, preferred_element_type=F32)
             for hc in range(2):
@@ -154,27 +203,42 @@
                 for c in range(4):
                     h_ref[o, hc, e, :, 128 * c:128 * c + 128] = hs[2 * e + hc, pl.ds(c, 256, stride=4), :].astype(BF)
 
-
-def spread(y, wy, wx, iy, ix, tab):
+    n_own = (n_buf[0] + (RUN - 1)) // RUN
+    n_nb = (jnp.sum(jnp.where(iy_ref[...] >= 0, 1.0, 0.0)).astype(jnp.int32) + (RUN - 1)) // RUN
+    for cp in copies:
+        cp.wait()
+    t_buf[0, :, GRID:] = -t_buf[1, :, :GRID]
+    payload(y_ref, wy_ref, wx_ref, iy_ref, ix_ref, pay)
+    ranks(iy_ref, oh, rank)
+
+    @pl.loop(0, n_nb)
+    def _(s):
+        d_nb[s] = reorder(s, pay, rank, pt)
+
+    block(0, d_own, n_own)
+    block(1, d_nb, n_nb)
+
+
+def spread(y, wy, wx, iy, ix, d_own, tab, n):
     vm = pl.BlockSpec(memory_space=pltpu.VMEM)
     return pl.pallas_call(
-        spread_kernel,
+        lambda *refs: spread_kernel(*refs[:7], *refs[8:10], refs[7], *refs[10:]),
         out_shape=(jax.ShapeDtypeStruct((2, 2, 2, 256, 512), BF), jax.ShapeDtypeStruct((2, 2, 64, 1024), F32)),
-        in_specs=[vm, vm, vm, vm, vm, pl.BlockSpec(memory_space=pl.ANY)],
+        in_specs=[vm, vm, vm, vm, vm, vm, pl.BlockSpec(memory_space=pl.ANY), pl.BlockSpec(memory_space=pltpu.SMEM)],
         out_specs=(vm, vm),
-        scratch_shapes=[
-            pltpu.VMEM((2112, 1024), F32),
-            pltpu.VMEM((2112, KC), BF),
-            pltpu.VMEM((1024, KC), BF),
-            pltpu.VMEM((1024, 2048), BF),
+        scratch_shapes=[pltpu.VMEM((SAMPLES // RUN, 160, RUN), BF)] + sort_scratch() + [
+            pltpu.VMEM((2, 16 * (66 + WIN), GRID), F32),
+            pltpu.VMEM((32 * WIN, RUN), BF),
+            pltpu.VMEM((GRID, RUN), BF),
+            pltpu.VMEM((1024, 2 * GRID), BF),
             pltpu.VMEM((4, 1024, 128), F32),
-            pltpu.VMEM((2, 256, 2048), BF),
+            pltpu.VMEM((2, 256, 2 * GRID), BF),
             pltpu.SemaphoreType.DMA((3,)),
         ],
         compiler_params=pltpu.CompilerParams(vmem_limit_bytes=40 * 2**20),
         cost_estimate=pl.CostEstimate(flops=13 * 10**9, bytes_accessed=4 * 2**20, transcendentals=0),
         name='spread',
-    )(y, wy, wx, iy, ix, tab)
+    )(y, wy, wx, iy, ix, d_own, tab, n)
 
 
 def combine_kernel(hh, ee, tab, maps, dd, out_ref,
@@ -344,7 +408,7 @@
         hbm = [pltpu.with_memory_space_constraint(v, pltpu.HBM) for v in (kspace, weight_row, weight_col, grid_row[None], grid_col[None])]
         stacked = exchange(*hbm, valid_count)
         tab = jnp.asarray(tables(n_img))
-        hh, ee = spread(*stacked, tab)
+        hh, ee = spread(*stacked, tab, valid_count)
         return combine(hh, ee, tab, coil_maps, deapod[None])
 
     spec_samples = P(None, 'coil', ('slab', 'rows'))

time: 49.4 us -> 45.1 us (0.913)
  Pallas kernels: 48.2 us -> 44.1 us
    pallas_call x2, Pallas kernels: 34.1 us -> 30 us  [the longest x1 20.6 us: spread(): pl.pallas_call(lambda *refs: spread_kernel(*refs[:7], *refs[8:10], refs[7...]
where the time goes in v3:
time: 45.1 us; the launch traced here: 45.7 us
  Pallas kernels  44.1 us (98%)
  between operations  0.87 us (2%)
  local copies, waits for them, and re-layouts  0.72 us (2%)
    pallas_call x1, Pallas kernels, spread(): pl.pallas_call(lambda *refs: spread_kernel(*refs[:7], *refs[8:10], refs[7...  20.6 us
    pallas_call x1, Pallas kernels, combine(): pl.pallas_call(combine_kernel, out_shape=jax.ShapeDtypeStruct((2, 256, 12...  14.1 us
    pallas_call x1, Pallas kernels, exchange(): pl.pallas_call(exchange_kernel, out_shape=tuple((jax.ShapeDtypeStruct(v.s...  9.44 us

profile of v3, /device:TPU:0, one launch (start us, length us, event | category | flops | bytes accessed | tf_op | source)
XLA Modules:
  0.0 45.7 jit_solution(3539961515577464796)
XLA Ops:
  0.0 0.0 copy-start.2
  0.8 9.4 %exchange.1 = (f32[2,4,2048]{2,1,0:T(4,128)S(1)}, f32[6,2048]{1,0:T(8,128)S(1)}, f32[6,2048]{1,0:T(8,128)S(1)}, s32[1,2048]{1,0:T(1,128)S(1)}, s32[1,2048]{1,0:T(1,128)S(1)}, /*index=5*/bf16[8,160,256]{2,1,0:T(8,128)(2,1)S(1)}) custom-call(f32[2,4,2048]{2,1,0:T(4,128)} %y_ref.1, f32[6,2048]{1,0:T(8,128)} %wy_ref.1, f32[6,2048]{1,0:T(8,128)} %wx_ref.1, ...), custom_call_target="tpu_custom_call" | custom-call | flops 1000000000 | bytes 1000000 | tf_op jit(solution)/shard_map/exchange/pallas_call | solution.py:139
  10.3 0.0 copy-done.2
  10.3 0.0 copy-start
  10.3 0.0 copy-start.1
  10.3 20.6 %spread.1 = (bf16[2,2,2,256,512]{4,3,2,1,0:T(8,128)(2,1)S(1)}, f32[2,2,64,1024]{3,2,1,0:T(8,128)S(1)}) custom-call(f32[2,4,2048]{2,1,0:T(4,128)S(1)} %get-tuple-element.13.refs_0_, f32[6,2048]{1,0:T(8,128)S(1)} %get-tuple-element.14.refs_1_, f32[6,2048]{1,0:T(8,128)S(1)} %get-tuple-element.15.refs_2_, s32[1,2048]{1,0:T(1,128)S(1)} %get-tuple-element.16.refs_3_, ...), custom_call_target="tpu_custom_call" | custom-call | flops 12999999488 | bytes 4194304 | tf_op jit(solution)/shard_map/spread/pallas_call | solution.py:224
  30.9 0.0 copy-done
  30.9 0.0 copy-done.1
  30.9 14.1 %combine.1 = f32[2,256,128]{2,1,0:T(8,128)S(1)} custom-call(bf16[2,2,2,256,512]{4,3,2,1,0:T(8,128)(2,1)S(1)} %get-tuple-element.19.hh, f32[2,2,64,1024]{3,2,1,0:T(8,128)S(1)} %get-tuple-element.20.ee, bf16[2,512,1024]{2,1,0:T(8,128)(2,1)S(1)} %copy-done.2, f32[2,4,512,128]{3,2,1,0:T(8,128)S(1)} %copy-done, f32[1,512]{1,0:T(1,128)S(1)} %bitcast.3), custom_call_target="tpu_custom_call" | custom-call | flops 3000000000 | bytes 12582912 | tf_op jit(solution)/shard_map/combine/pallas_call | solution.py:380
  45.0 0.7 %copy.12 = f32[2,256,128]{2,1,0:T(8,128)} copy(f32[2,256,128]{2,1,0:T(8,128)S(1)} %combine.1) | data formatting | bytes 524288
Async XLA Ops:
  0.0 10.3 %copy-start.2 = (bf16[2,512,1024]{2,1,0:T(8,128)(2,1)S(1)}, bf16[2,512,1024]{2,1,0:T(8,128)(2,1)}, u32[]{:S(2)}) copy-start(bf16[2,512,1024]{2,1,0:T(8,128)(2,1)} %constant.2.clone.refs_6_.tab) | copy-start | bytes 6291460
  10.3 20.6 %copy-start = (f32[2,4,512,128]{3,2,1,0:T(8,128)S(1)}, f32[2,4,512,128]{3,2,1,0:T(8,128)}, u32[]{:S(2)}) copy-start(f32[2,4,512,128]{3,2,1,0:T(8,128)} %maps.1) | copy-start | bytes 6291460
  10.3 20.6 %copy-start.1 = (f32[512]{0:T(512)S(1)}, f32[512]{0:T(512)}, u32[]{:S(2)}) copy-start(f32[512]{0:T(512)} %param.16) | copy-start | bytes 6148

commit v4 on v3

--- a/solution.py
+++ b/solution.py
@@ -148,17 +148,7 @@
     )(y, wy, wx, iy, ix, n)
 
 
-def spread_kernel(y_ref, wy_ref, wx_ref, iy_ref, ix_ref, d_own, tab, h_ref, e_ref,
-                  n_buf, d_nb, pay, oh, rank, pt, acc, a_buf, b_buf, g_buf, hs, t_buf, sem):
-    x_id = lax.axis_index('rows') // 2
-    my_cols = pl.ds(pl.multiple_of(x_id * 256, 256), 256)
-    copies = [
-        pltpu.make_async_copy(tab.at[0, my_cols], t_buf.at[0, :, pl.ds(0, GRID)], sem.at[0]),
-        pltpu.make_async_copy(tab.at[1, my_cols], t_buf.at[1, :, pl.ds(0, GRID)], sem.at[1]),
-        pltpu.make_async_copy(tab.at[0, my_cols], t_buf.at[1, :, pl.ds(GRID, GRID)], sem.at[2]),
-    ]
-    for cp in copies:
-        cp.start()
+def spread_kernel(y_ref, wy_ref, wx_ref, iy_ref, ix_ref, d_own, n_ref, g_ref, e_ref, d_nb, pay, oh, rank, pt, acc, a_buf, b_buf):
     zero = jnp.zeros((16, RUN), BF)
 
     def run(d_ref, s):
@@ -193,21 +183,10 @@
         for q in range(2):
             e_ref[o, q, 0:32] = acc[q, 0:32, :]
             e_ref[o, q, 32:64] = acc[q, 1024:1056, :]
-            g_buf[:, GRID * q:GRID * (q + 1)] = acc[q, 16:1040, :].astype(BF)
-        for e in range(2):
-            prod = lax.dot_general(g_buf[...], t_buf[e], NT, preferred_element_type=F32)
-            for hc in range(2):
-                hs[2 * e + hc] = prod[:, 128 * hc:128 * hc + 128]
-        for e in range(2):
-            for hc in range(2):
-                for c in range(4):
-                    h_ref[o, hc, e, :, 128 * c:128 * c + 128] = hs[2 * e + hc, pl.ds(c, 256, stride=4), :].astype(BF)
-
-    n_own = (n_buf[0] + (RUN - 1)) // RUN
+            g_ref[o, :, GRID * q:GRID * (q + 1)] = acc[q, 16:1040, :].astype(BF)
+
+    n_own = (n_ref[0] + (RUN - 1)) // RUN
     n_nb = (jnp.sum(jnp.where(iy_ref[...] >= 0, 1.0, 0.0)).astype(jnp.int32) + (RUN - 1)) // RUN
-    for cp in copies:
-        cp.wait()
-    t_buf[0, :, GRID:] = -t_buf[1, :, :GRID]
     payload(y_ref, wy_ref, wx_ref, iy_ref, ix_ref, pay)
     ranks(iy_ref, oh, rank)
 
@@ -219,64 +198,47 @@
     block(1, d_nb, n_nb)
 
 
-def spread(y, wy, wx, iy, ix, d_own, tab, n):
+def spread(y, wy, wx, iy, ix, d_own, n):
     vm = pl.BlockSpec(memory_space=pltpu.VMEM)
     return pl.pallas_call(
-        lambda *refs: spread_kernel(*refs[:7], *refs[8:10], refs[7], *refs[10:]),
-        out_shape=(jax.ShapeDtypeStruct((2, 2, 2, 256, 512), BF), jax.ShapeDtypeStruct((2, 2, 64, 1024), F32)),
-        in_specs=[vm, vm, vm, vm, vm, vm, pl.BlockSpec(memory_space=pl.ANY), pl.BlockSpec(memory_space=pltpu.SMEM)],
+        spread_kernel,
+        out_shape=(jax.ShapeDtypeStruct((2, 1024, 2 * GRID), BF), jax.ShapeDtypeStruct((2, 2, 64, GRID), F32)),
+        in_specs=[vm, vm, vm, vm, vm, vm, pl.BlockSpec(memory_space=pltpu.SMEM)],
         out_specs=(vm, vm),
         scratch_shapes=[pltpu.VMEM((SAMPLES // RUN, 160, RUN), BF)] + sort_scratch() + [
             pltpu.VMEM((2, 16 * (66 + WIN), GRID), F32),
             pltpu.VMEM((32 * WIN, RUN), BF),
             pltpu.VMEM((GRID, RUN), BF),
-            pltpu.VMEM((1024, 2 * GRID), BF),
-            pltpu.VMEM((4, 1024, 128), F32),
-            pltpu.VMEM((2, 256, 2 * GRID), BF),
-            pltpu.SemaphoreType.DMA((3,)),
         ],
-        compiler_params=pltpu.CompilerParams(vmem_limit_bytes=40 * 2**20),
+        compiler_params=pltpu.CompilerParams(vmem_limit_bytes=28 * 2**20),
         cost_estimate=pl.CostEstimate(flops=13 * 10**9, bytes_accessed=4 * 2**20, transcendentals=0),
         name='spread',
-    )(y, wy, wx, iy, ix, d_own, tab, n)
-
-
-def combine_kernel(hh, ee, tab, maps, dd, out_ref,
-                   t3, rhs, sbuf, s_vm, rx, ge, hs, pt, part, rx2, scale,
-                   loc, esend, erecv, hsend, hrecv, psend, precv, ysend, yrecv):
-    n_grid = 1024
+    )(y, wy, wx, iy, ix, d_own, n)
+
+
+def combine_kernel(gg, ee, tab, maps, dd, out_ref, hbuf, hs, ge, rx, s_all, part, rx2, scale,
+                   esend, erecv, ssem, hsend, hrecv, ysend, yrecv):
     row_id = lax.axis_index('rows')
     y_id = lax.axis_index('coil')
     core = row_id % 2
     x_id = row_id // 2
-    sib = {'rows': row_id + 1 - 2 * core}
-    mate = {'coil': 1 - y_id}
+    sib_row = row_id + 1 - 2 * core
+    sib = {'rows': sib_row}
+    mate = {'coil': 1 - y_id, 'rows': sib_row}
     blocks = [row_id, (row_id + 2) % 4]
-
-    n_loc = 0
-    t_copies = []
-    for src, dst in ((tab.at[0], t3.at[0, :, pl.ds(0, n_grid)]), (tab.at[1], t3.at[1, :, pl.ds(0, n_grid)]), (tab.at[0], t3.at[1, :, pl.ds(n_grid, n_grid)])):
-        t_copies.append(pltpu.make_async_copy(src, dst, loc.at[n_loc]))
-        n_loc += 1
-    h_copies = []
-    for o in range(2):
-        for b in range(2):
-            h_copies.append(pltpu.make_async_copy(hh.at[o, core, b], rhs.at[b, blocks[o]], loc.at[n_loc]))
-            n_loc += 1
-            for end in range(2):
-                h_copies.append(pltpu.make_async_copy(hh.at[o, 1 - core, b, pl.ds(240 * end, 16)], sbuf.at[o, b, end], loc.at[n_loc]))
-                n_loc += 1
-    s_copy = pltpu.make_async_copy(maps, s_vm, loc.at[n_loc])
-    for cp in t_copies + h_copies:
-        cp.start()
 
     barrier = pltpu.get_barrier_semaphore()
     pl.semaphore_signal(barrier, inc=1, device_id=sib, device_id_type=pl.DeviceIdType.MESH)
     pl.semaphore_signal(barrier, inc=1, device_id=mate, device_id_type=pl.DeviceIdType.MESH)
+    half = lambda y: pl.ds(pl.multiple_of(y * 256, 256), 256)
+    s_copy = pltpu.make_async_copy(maps.at[:, :, half(y_id)], s_all.at[core], ssem.at[0])
+    s_copy.start()
+    row_scale = jnp.broadcast_to(dd[:, half(y_id)], (128, 256)).T
+    scale[...] = row_scale * dd[:, pl.ds(pl.multiple_of(row_id * 128, 128), 128)]
     pl.semaphore_wait(barrier, 2)
 
-    def remote(src, dst, ssem, rsem, dev):
-        return pltpu.make_async_remote_copy(src_ref=src, dst_ref=dst, send_sem=ssem, recv_sem=rsem, device_id=dev, device_id_type=pl.DeviceIdType.MESH)
+    def remote(src, dst, send, recv, dev):
+        return pltpu.make_async_remote_copy(src_ref=src, dst_ref=dst, send_sem=send, recv_sem=recv, device_id=dev, device_id_type=pl.DeviceIdType.MESH)
 
     e_copies = []
     for o in range(2):
@@ -286,120 +248,125 @@
             e_copies.append(remote(ee.at[o, :, pl.ds(row0, 16)], rx.at[slot, end], esend.at[2 * o + k], erecv.at[slot, end], sib))
     for cp in e_copies:
         cp.start()
-    hr_copies = []
+    s_send = remote(maps.at[:, :, half(1 - y_id)], s_all.at[core], ssem.at[1], ssem.at[2], sib)
+    s_send.start()
+    s_recv = remote(maps.at[:, :, half(1 - y_id)], s_all.at[1 - core], ssem.at[1], ssem.at[2], sib)
+
+    def columns(hc, lhs):
+        cols = pl.ds(pl.multiple_of(x_id * 256 + hc * 128, 128), 128)
+        t2 = jnp.concatenate([tab[0, cols, :], tab[1, cols, :]], axis=0)
+        pr = lax.dot_general(lhs(0), t2, NT, preferred_element_type=F32)
+        pi = lax.dot_general(lhs(1), t2, NT, preferred_element_type=F32)
+        return pr[:, :128] - pi[:, 128:], pr[:, 128:] + pi[:, :128]
+
+    def transform(hc, o):
+        for k in range(2):
+            rows = slice(512 * k, 512 * k + 512)
+            pair = columns(hc, lambda q: gg[o, rows, GRID * q:GRID * (q + 1)])
+            for e in range(2):
+                hs[o, e, rows] = pair[e]
+
+    def take_halos():
+        for cp in e_copies:
+            cp.wait_send()
+        for o in range(2):
+            for end in range(2):
+                remote(rx.at[o, end], rx.at[o, end], esend.at[2 * o + end], erecv.at[o, end], sib).wait_recv()
+                for q in range(2):
+                    ge[32 * o + 16 * end:32 * o + 16 * end + 16, GRID * q:GRID * (q + 1)] = (ee[o, q, 16 + 16 * end:32 + 16 * end, :] + rx[o, end, q]).astype(BF)
+
+    def patch(hc):
+        pair = columns(hc, lambda q: ge[:, GRID * q:GRID * (q + 1)])
+        return pair
+
+    h_copies = [[remote(hbuf.at[hc, blocks[o]], hbuf.at[hc, blocks[o]], hsend.at[hc, o], hrecv.at[hc, o], sib) for o in range(2)] for hc in range(2)]
+
+    def send(hc, o, pair):
+        for e in range(2):
+            for end in range(2):
+                hs[o, e, 1008 * end:1008 * end + 16] = pair[e][32 * o + 16 * end:32 * o + 16 * end + 16]
+            for c in range(4):
+                hbuf[hc, blocks[o], e, :, 128 * c:128 * c + 128] = hs[o, e, pl.ds(c, 256, stride=4), :].astype(BF)
+        h_copies[hc][o].start()
+
+    def image(hc):
+        first = 256 * (y_id + (1 - 2 * y_id) * (core + hc - 2 * core * hc))
+        for k in range(2):
+            rows = pl.ds(pl.multiple_of(first + 128 * k, 128), 128)
+            lhs = jnp.concatenate([tab[0, rows, :], tab[1, rows, :]], axis=0)
+            mr = jnp.dot(lhs, hbuf[hc, :, 0].reshape(1024, 512), preferred_element_type=F32)
+            mi = jnp.dot(lhs, hbuf[hc, :, 1].reshape(1024, 512), preferred_element_type=F32)
+            re = mr[:128] - mi[128:]
+            im = mr[128:] + mi[:128]
+            xr = jnp.zeros((128, 128), F32)
+            xi = jnp.zeros((128, 128), F32)
+            sl = slice(128 * k, 128 * k + 128)
+            for c in range(4):
+                ir = re[:, 128 * c:128 * c + 128]
+                ii = im[:, 128 * c:128 * c + 128]
+                sr = s_all[hc, 0, c, sl, :]
+                si = s_all[hc, 1, c, sl, :]
+                xr = xr + (sr * ir + si * ii)
+                xi = xi + (sr * ii - si * ir)
+            part[hc, 0, sl] = xr
+            part[hc, 1, sl] = xi
+
+            @pl.when(core != hc)
+            def _():
+                y_copies[k].start()
+
+    y_copies = [remote(part.at[1 - core, :, pl.ds(128 * k, 128)], rx2.at[:, pl.ds(128 * k, 128)], ysend.at[k], yrecv.at[k], mate) for k in range(2)]
+
+    transform(0, 0)
+    take_halos()
+    pair = patch(0)
+    send(0, 0, pair)
+    transform(0, 1)
+    send(0, 1, pair)
+    transform(1, 0)
+    pair = patch(1)
+    send(1, 0, pair)
+    s_copy.wait()
+    s_send.wait_send()
+    s_recv.wait_recv()
     for o in range(2):
-        for b in range(2):
-            hr_copies.append(remote(hh.at[o, 1 - core, b, pl.ds(16, 224)], rhs.at[b, blocks[o], pl.ds(16, 224)], hsend.at[o, b], hrecv.at[o, b], sib))
-    for cp in hr_copies:
-        cp.start()
-    s_copy.start()
-    row_scale = jnp.broadcast_to(dd[:, pl.ds(pl.multiple_of(y_id * 256, 256), 256)], (128, 256)).T
-    scale[...] = row_scale * dd[:, pl.ds(pl.multiple_of(row_id * 128, 128), 128)]
-
-    for cp in t_copies:
-        cp.wait()
-    t3[0, :, n_grid:] = -t3[1, :, :n_grid]
-    for cp in e_copies:
-        cp.wait_send()
+        h_copies[0][o].wait()
+    image(0)
+    transform(1, 1)
+    send(1, 1, pair)
     for o in range(2):
-        for end in range(2):
-            remote(rx.at[o, end], rx.at[o, end], esend.at[2 * o + end], erecv.at[o, end], sib).wait_recv()
-            for q in range(2):
-                ge[32 * o + 16 * end:32 * o + 16 * end + 16, n_grid * q:n_grid * (q + 1)] = (ee[o, q, 16 + 16 * end:32 + 16 * end, :] + rx[o, end, q]).astype(BF)
-    cols = pl.ds(pl.multiple_of(x_id * 256, 256), 256)
-    for e in range(2):
-        prod = lax.dot_general(ge[...], t3[e, cols, :], NT, preferred_element_type=F32)
-        for hc in range(2):
-            hs[2 * e + hc] = prod[:, 128 * hc:128 * hc + 128]
-    for cp in h_copies:
-        cp.wait()
-    p_copies = []
-    n_p = 0
-    for o in range(2):
-        for end in range(2):
-            for b in range(2):
-                for mine in range(2):
-                    hc = core if mine else 1 - core
-                    rows = pl.ds(240 * end, 16)
-                    if mine:
-                        pt[...] = rhs[b, blocks[o], rows, :].astype(F32)
-                    else:
-                        pt[...] = sbuf[o, b, end].astype(F32)
-                    for c in range(4):
-                        pt[12 * end:12 * end + 4, 128 * c:128 * c + 128] = hs[2 * b + hc, pl.ds(32 * o + 16 * end + c, 4, stride=4), :]
-                    if mine:
-                        rhs[b, blocks[o], rows, :] = pt[...].astype(BF)
-                    else:
-                        sbuf[o, b, end] = pt[...].astype(BF)
-                        cp = remote(sbuf.at[o, b, end], rhs.at[b, blocks[o], rows], psend.at[n_p], precv.at[n_p], sib)
-                        cp.start()
-                        p_copies.append(cp)
-                        n_p += 1
-    s_copy.wait()
-    for cp in hr_copies + p_copies:
-        cp.wait()
-
-    def image_rows(i0, size):
-        rows = pl.ds(pl.multiple_of(i0, size), size)
-        w = rhs[...].reshape(2048, 512)
-        im = [jnp.dot(t3[e, rows, :], w, preferred_element_type=F32) for e in range(2)]
-        xr = jnp.zeros((size, 128), F32)
-        xi = jnp.zeros((size, 128), F32)
-        for c in range(4):
-            ir = im[0][:, 128 * c:128 * c + 128]
-            ii = im[1][:, 128 * c:128 * c + 128]
-            sr = s_vm[0, c, rows, :]
-            si = s_vm[1, c, rows, :]
-            xr = xr + (sr * ir + si * ii)
-            xi = xi + (sr * ii - si * ir)
-        return xr, xi
-
-    y_copies = []
-    for k in range(2):
-        xr, xi = image_rows((1 - y_id) * 256 + 128 * k, 128)
-        part[0, 128 * k:128 * k + 128] = xr
-        part[1, 128 * k:128 * k + 128] = xi
-        cp = remote(part.at[:, pl.ds(128 * k, 128)], rx2.at[:, pl.ds(128 * k, 128)], ysend.at[k], yrecv.at[k], mate)
-        cp.start()
-        y_copies.append(cp)
-    for k in range(2):
-        xr, xi = image_rows(y_id * 256 + 128 * k, 128)
-        out_ref[0, 128 * k:128 * k + 128] = xr
-        out_ref[1, 128 * k:128 * k + 128] = xi
+        h_copies[1][o].wait()
+    image(1)
     for k in range(2):
         y_copies[k].wait()
         sl = slice(128 * k, 128 * k + 128)
         for e in range(2):
-            out_ref[e, sl] = (out_ref[e, sl] + rx2[e, sl]) * scale[sl]
-
-
-def combine(hh, ee, tab, maps, dd):
+            out_ref[e, sl] = (part[core, e, sl] + rx2[e, sl]) * scale[sl]
+
+
+def combine(gg, ee, tab, maps, dd):
     vm = pl.BlockSpec(memory_space=pltpu.VMEM)
-    anym = pl.BlockSpec(memory_space=pl.ANY)
     dma = pltpu.SemaphoreType.DMA
     return pl.pallas_call(
         combine_kernel,
         out_shape=jax.ShapeDtypeStruct((2, 256, 128), F32),
-        in_specs=[anym, vm, anym, anym, vm],
+        in_specs=[vm] * 5,
         out_specs=vm,
         scratch_shapes=[
-            pltpu.VMEM((2, 512, 2048), BF),
-            pltpu.VMEM((2, 4, 256, 512), BF),
-            pltpu.VMEM((2, 2, 2, 16, 512), BF),
-            pltpu.VMEM((2, 4, 512, 128), F32),
-            pltpu.VMEM((2, 2, 2, 16, 1024), F32),
-            pltpu.VMEM((64, 2048), BF),
-            pltpu.VMEM((4, 64, 128), F32),
-            pltpu.VMEM((16, 512), F32),
-            pltpu.VMEM((2, 256, 128), F32),
+            pltpu.VMEM((2, 4, 2, 256, 512), BF),
+            pltpu.VMEM((2, 2, 1024, 128), F32),
+            pltpu.VMEM((64, 2 * GRID), BF),
+            pltpu.VMEM((2, 2, 2, 16, GRID), F32),
+            pltpu.VMEM((2, 2, 4, 256, 128), F32),
+            pltpu.VMEM((2, 2, 256, 128), F32),
             pltpu.VMEM((2, 256, 128), F32),
             pltpu.VMEM((256, 128), F32),
-            dma((16,)), dma((4,)), dma((2, 2)), dma((2, 2)), dma((2, 2)), dma((8,)), dma((8,)), dma((2,)), dma((2,)),
+            dma((4,)), dma((2, 2)), dma((3,)), dma((2, 2)), dma((2, 2)), dma((2,)), dma((2,)),
         ],
-        compiler_params=pltpu.CompilerParams(vmem_limit_bytes=40 * 2**20, collective_id=0, has_side_effects=True),
-        cost_estimate=pl.CostEstimate(flops=3 * 10**9, bytes_accessed=12 * 2**20, transcendentals=0),
+        compiler_params=pltpu.CompilerParams(vmem_limit_bytes=24 * 2**20, collective_id=0, has_side_effects=True),
+        cost_estimate=pl.CostEstimate(flops=7 * 10**9, bytes_accessed=12 * 2**20, transcendentals=0),
         name='combine',
-    )(hh, ee, tab, maps, dd)
+    )(gg, ee, tab, maps, dd)
 
 
 def solution(mesh):
@@ -408,8 +375,8 @@
         hbm = [pltpu.with_memory_space_constraint(v, pltpu.HBM) for v in (kspace, weight_row, weight_col, grid_row[None], grid_col[None])]
         stacked = exchange(*hbm, valid_count)
         tab = jnp.asarray(tables(n_img))
-        hh, ee = spread(*stacked, tab, valid_count)
-        return combine(hh, ee, tab, coil_maps, deapod[None])
+        gg, ee = spread(*stacked, valid_count)
+        return combine(gg, ee, tab, coil_maps, deapod[None])
 
     spec_samples = P(None, 'coil', ('slab', 'rows'))
     spec_weights = P(None, ('slab', 'rows'))

time: 45.1 us -> 43.6 us (0.967); the launches traced: 45.7 us -> 43.5 us
  Pallas kernels: 44.1 us -> 42 us
    pallas_call x1, Pallas kernels: 20.6 us -> 16.6 us  [spread(): pl.pallas_call(spread_kernel, out_shape=(jax.ShapeDtypeStruct((2, 1024, 2...]
    pallas_call x1, Pallas kernels: 14.1 us -> 16 us  [combine(): pl.pallas_call(combine_kernel, out_shape=jax.ShapeDtypeStruct((2, 256, 12...]
where the time goes in v4:
time: 43.6 us; the launch traced here: 43.5 us
  Pallas kernels  42 us (96%)
  local copies, waits for them, and re-layouts  0.72 us (2%)
  between operations  0.72 us (2%)
    pallas_call x1, Pallas kernels, spread(): pl.pallas_call(spread_kernel, out_shape=(jax.ShapeDtypeStruct((2, 1024, 2...  16.6 us
    pallas_call x1, Pallas kernels, combine(): pl.pallas_call(combine_kernel, out_shape=jax.ShapeDtypeStruct((2, 256, 12...  16 us
    pallas_call x1, Pallas kernels, exchange(): pl.pallas_call(exchange_kernel, out_shape=tuple((jax.ShapeDtypeStruct(v.s...  9.44 us

profile of v4, /device:TPU:0, one launch (start us, length us, event | category | flops | bytes accessed | tf_op | source)
XLA Modules:
  0.0 43.5 jit_solution(10680899769964310918)
XLA Ops:
  0.7 9.4 %exchange.1 = (f32[2,4,2048]{2,1,0:T(4,128)S(1)}, f32[6,2048]{1,0:T(8,128)S(1)}, f32[6,2048]{1,0:T(8,128)S(1)}, s32[1,2048]{1,0:T(1,128)S(1)}, s32[1,2048]{1,0:T(1,128)S(1)}, /*index=5*/bf16[8,160,256]{2,1,0:T(8,128)(2,1)S(1)}) custom-call(f32[2,4,2048]{2,1,0:T(4,128)} %y_ref.1, f32[6,2048]{1,0:T(8,128)} %wy_ref.1, f32[6,2048]{1,0:T(8,128)} %wx_ref.1, ...), custom_call_target="tpu_custom_call" | custom-call | flops 1000000000 | bytes 1000000 | tf_op jit(solution)/shard_map/exchange/pallas_call | solution.py:139
  10.1 0.0 copy-start
  10.1 0.0 copy-start.1
  10.1 0.0 copy-start.2
  10.1 16.6 %spread.1 = (bf16[2,1024,2048]{2,1,0:T(8,128)(2,1)S(1)}, f32[2,2,64,1024]{3,2,1,0:T(8,128)S(1)}) custom-call(f32[2,4,2048]{2,1,0:T(4,128)S(1)} %get-tuple-element.13.y_ref, f32[6,2048]{1,0:T(8,128)S(1)} %get-tuple-element.14.wy_ref, f32[6,2048]{1,0:T(8,128)S(1)} %get-tuple-element.15.wx_ref, s32[1,2048]{1,0:T(1,128)S(1)} %get-tuple-element.16.iy_ref, ...), custom_call_target="tpu_custom_call" | custom-call | flops 12999999488 | bytes 4194304 | tf_op jit(solution)/shard_map/spread/pallas_call | solution.py:203
  26.7 0.0 copy-done
  26.7 0.0 copy-done.1
  26.7 0.0 copy-done.2
  26.7 16.0 %combine.1 = f32[2,256,128]{2,1,0:T(8,128)S(1)} custom-call(bf16[2,1024,2048]{2,1,0:T(8,128)(2,1)S(1)} %get-tuple-element.19.gg, f32[2,2,64,1024]{3,2,1,0:T(8,128)S(1)} %get-tuple-element.20.ee, bf16[2,512,1024]{2,1,0:T(8,128)(2,1)S(1)} %copy-done.2, f32[2,4,512,128]{3,2,1,0:T(8,128)S(1)} %copy-done, f32[1,512]{1,0:T(1,128)S(1)} %bitcast.3), custom_call_target="tpu_custom_call" | custom-call | flops 7000000000 | bytes 12582912 | tf_op jit(solution)/shard_map/combine/pallas_call | solution.py:350
  42.8 0.7 %copy.12 = f32[2,256,128]{2,1,0:T(8,128)} copy(f32[2,256,128]{2,1,0:T(8,128)S(1)} %combine.1) | data formatting | bytes 524288
Async XLA Ops:
  10.1 16.6 %copy-start = (f32[2,4,512,128]{3,2,1,0:T(8,128)S(1)}, f32[2,4,512,128]{3,2,1,0:T(8,128)}, u32[]{:S(2)}) copy-start(f32[2,4,512,128]{3,2,1,0:T(8,128)} %maps.1) | copy-start | bytes 6291460
  10.1 16.6 %copy-start.1 = (f32[512]{0:T(512)S(1)}, f32[512]{0:T(512)}, u32[]{:S(2)}) copy-start(f32[512]{0:T(512)} %param.16) | copy-start | bytes 6148
  10.1 16.6 %copy-start.2 = (bf16[2,512,1024]{2,1,0:T(8,128)(2,1)S(1)}, bf16[2,512,1024]{2,1,0:T(8,128)(2,1)}, u32[]{:S(2)}) copy-start(bf16[2,512,1024]{2,1,0:T(8,128)(2,1)} %constant.2.clone.tab) | copy-start | bytes 6291460

commit v5 on v4

--- a/solution.py
+++ b/solution.py
@@ -15,7 +15,7 @@
 GRID = 1024
 SAMPLES = 2048
 RUN = 256
-WIN = 12
+WIN = 16
 
 
 def tables(n_img):
@@ -26,12 +26,13 @@
     return np.stack([np.cos(ang), np.sin(ang)]).astype(np.float32).astype(BF)
 
 
-def payload(y_ref, wy_ref, wx_ref, iy_ref, ix_ref, pay):
+def payload(y_ref, wy_ref, wx_ref, key_ref, pay):
     @pl.loop(0, SAMPLES // KC)
     def _(s):
         cols = pl.ds(pl.multiple_of(s * KC, KC), KC)
         sub = lax.broadcasted_iota(jnp.int32, (16, KC), 0)
-        r0 = iy_ref[:, cols] + 1
+        key = key_ref[:, cols]
+        r0 = (key >> 10) + 1
         counted = r0 > 0
         t = jnp.where(counted, (sub >> 2) - (r0 & 3), 100)
         for q in range(2):
@@ -45,12 +46,13 @@
                     if -3 <= a - 4 * j <= 3:
                         e = jnp.where(t == a - 4 * j, coef[a], e)
                 pay[48 * q + 16 * j:48 * q + 16 * j + 16, cols] = e.astype(BF)
-        c0 = (ix_ref[:, cols] + (GRID - 3)) & (GRID - 1)
+        c0 = ((key & (GRID - 1)) + (GRID - 3)) & (GRID - 1)
+        wx = wx_ref[:, cols].astype(F32)
         tc = jnp.where(counted, sub - (c0 & 15), 100)
         for j in range(2):
             e = jnp.zeros((16, KC), F32)
             for b in range(6):
-                e = jnp.where(tc == b - 16 * j, wx_ref[b:b + 1, cols], e)
+                e = jnp.where(tc == b - 16 * j, wx[b:b + 1], e)
             pay[96 + 16 * j:112 + 16 * j, cols] = e.astype(BF)
         pay[128:144, cols] = jnp.broadcast_to(((r0 >> 2) + 1).astype(F32), (16, KC)).astype(BF)
         pay[144:160, cols] = jnp.broadcast_to((c0 >> 4).astype(F32), (16, KC)).astype(BF)
@@ -60,11 +62,11 @@
     return lax.broadcasted_iota(jnp.int32, (16, 1), 0).astype(F32)
 
 
-def ranks(iy_ref, oh, rank):
+def ranks(key_ref, oh, rank):
     n_run = SAMPLES // RUN
     for ch in range(n_run):
         lanes = slice(RUN * ch, RUN * ch + RUN)
-        bucket = jnp.broadcast_to(((iy_ref[:, lanes] + 1) >> 2).astype(F32), (16, RUN)).astype(BF)
+        bucket = jnp.broadcast_to((((key_ref[:, lanes] >> 10) + 1) >> 2).astype(F32), (16, RUN)).astype(BF)
         for g in range(5):
             oh[80 * ch + 16 * g:80 * ch + 16 * g + 16, :] = jnp.where(bucket == (iota16() + 16 * g).astype(BF), jnp.ones((), BF), jnp.zeros((), BF))
     lower = lax.broadcasted_iota(jnp.int32, (RUN, RUN + 128), 0)
@@ -83,41 +85,49 @@
         lanes = slice(RUN * ch, RUN * ch + RUN)
         place = pre[80 * ch:80 * ch + 80, :RUN] + jnp.concatenate([base] * (RUN // 128), axis=1)
         place = jnp.sum(oh[80 * ch:80 * ch + 80, :].astype(F32) * place, axis=0, keepdims=True)
-        rank[:, lanes] = jnp.where(iy_ref[:, lanes] >= 0, place, -1.0)
+        place = jnp.where(key_ref[:, lanes] >= 0, place, -1.0)
+        for k in range(RUN // 128):
+            rank[RUN * ch + 128 * k:RUN * ch + 128 * k + 128, :] = jnp.broadcast_to(place[:, 128 * k:128 * k + 128], (128, 128)).T
         base = base + counts[ch]
 
 
 def reorder(s, pay, rank, pt):
-    place = jnp.broadcast_to(rank[...] - (s * RUN).astype(F32), (16, SAMPLES)).astype(BF)
-    for g in range(RUN // 16):
-        pt[16 * g:16 * g + 16, :] = jnp.where(place == (iota16() + 16 * g).astype(BF), jnp.ones((), BF), jnp.zeros((), BF))
-    return lax.dot_general(pay[...], pt[...], NT, preferred_element_type=F32).astype(BF)
-
-
-def exchange_kernel(y_ref, wy_ref, wx_ref, iy_ref, ix_ref, n_ref, y_out, wy_out, wx_out, iy_out, ix_out, d_out,
-                    y_in, wy_in, wx_in, iy_in, ix_in, iy_raw, pay, oh, rank, pt, loc, ssem, rsem):
+    lane = lax.broadcasted_iota(jnp.int32, (1, 128), 1).astype(F32)
+    one, zero = jnp.ones((), BF), jnp.zeros((), BF)
+    for t in range(SAMPLES // 128):
+        rows = slice(128 * t, 128 * t + 128)
+        place = (rank[rows, :] - (s * RUN).astype(F32)).astype(BF)
+        for k in range(RUN // 128):
+            pt[rows, 128 * k:128 * k + 128] = jnp.where(place == (lane + 128 * k).astype(BF), one, zero)
+    return jnp.dot(pay[...], pt[...], preferred_element_type=F32).astype(BF)
+
+
+def exchange_kernel(y_ref, wy_ref, wx_ref, iy_ref, ix_ref, n_ref, y_out, wy_out, wx_out, key_out, key_own, d_out,
+                    y_in, wy_in, wx_in, iy_in, ix_in, wx_bf, pay, oh, rank, pt, loc, ssem, rsem):
     row_id = lax.axis_index('rows')
     other = {'rows': (row_id + 2) % 4}
-    iy_copy = pltpu.make_async_copy(iy_ref, iy_raw, loc.at[4])
-    iy_copy.start()
-    trips = [(y_ref, y_in, y_out), (wy_ref, wy_in, wy_out), (wx_ref, wx_in, wx_out), (ix_ref, ix_in, ix_out)]
-    locs = [pltpu.make_async_copy(a, b, loc.at[i]) for i, (a, b, _) in enumerate(trips)]
+    barrier = pltpu.get_barrier_semaphore()
+    pl.semaphore_signal(barrier, inc=1, device_id=other, device_id_type=pl.DeviceIdType.MESH)
+    pairs = [(iy_ref, iy_in), (ix_ref, ix_in), (wx_ref, wx_in), (wy_ref, wy_in), (y_ref, y_in)]
+    locs = [pltpu.make_async_copy(a, b, loc.at[i]) for i, (a, b) in enumerate(pairs)]
     for cp in locs:
         cp.start()
-    barrier = pltpu.get_barrier_semaphore()
-    pl.semaphore_signal(barrier, inc=1, device_id=other, device_id_type=pl.DeviceIdType.MESH)
-    iy_copy.wait()
+    moves = [(y_ref, y_out), (wy_ref, wy_out), (key_own, key_out), (wx_bf, wx_out)]
+    sends = [pltpu.make_async_remote_copy(src_ref=a, dst_ref=b, send_sem=ssem.at[i], recv_sem=rsem.at[i], device_id=other, device_id_type=pl.DeviceIdType.MESH) for i, (a, b) in enumerate(moves)]
+    pl.semaphore_wait(barrier, 1)
+    sends[0].start()
+    sends[1].start()
+    for cp in locs[:3]:
+        cp.wait()
     slot = lax.broadcasted_iota(jnp.int32, iy_in.shape, 1)
-    iy_in[...] = jnp.where(slot < n_ref[0], iy_raw[...] - row_id * 256, -1000)
-    pl.semaphore_wait(barrier, 1)
-    trips.append((iy_in, None, iy_out))
-    sends = [pltpu.make_async_remote_copy(src_ref=a, dst_ref=b, send_sem=ssem.at[i], recv_sem=rsem.at[i], device_id=other, device_id_type=pl.DeviceIdType.MESH) for i, (a, _, b) in enumerate(trips)]
-    for cp in sends:
-        cp.start()
-    for cp in locs:
-        cp.wait()
-    payload(y_in, wy_in, wx_in, iy_in, ix_in, pay)
-    ranks(iy_in, oh, rank)
+    key_own[...] = jnp.where(slot < n_ref[0], (iy_in[...] - row_id * 256) * GRID + ix_in[...], -1000 * GRID)
+    wx_bf[...] = wx_in[...].astype(BF)
+    sends[2].start()
+    sends[3].start()
+    for cp in locs[3:]:
+        cp.wait()
+    payload(y_in, wy_in, wx_bf, key_own, pay)
+    ranks(key_own, oh, rank)
 
     @pl.loop(0, SAMPLES // RUN)
     def _(s):
@@ -128,27 +138,27 @@
 
 
 def sort_scratch():
-    return [pltpu.VMEM((160, SAMPLES), BF), pltpu.VMEM((80 * (SAMPLES // RUN), RUN), BF), pltpu.VMEM((1, SAMPLES), F32), pltpu.VMEM((RUN, SAMPLES), BF)]
+    return [pltpu.VMEM((160, SAMPLES), BF), pltpu.VMEM((80 * (SAMPLES // RUN), RUN), BF), pltpu.VMEM((SAMPLES, 128), F32), pltpu.VMEM((SAMPLES, RUN), BF)]
 
 
 def exchange(y, wy, wx, iy, ix, n):
     vm = pl.BlockSpec(memory_space=pltpu.VMEM)
     anym = pl.BlockSpec(memory_space=pl.ANY)
     dma = pltpu.SemaphoreType.DMA
-    raw = (y, wy, wx, iy, ix)
+    shape = jax.ShapeDtypeStruct
     return pl.pallas_call(
         exchange_kernel,
-        out_shape=tuple(jax.ShapeDtypeStruct(v.shape, v.dtype) for v in raw) + (jax.ShapeDtypeStruct((SAMPLES // RUN, 160, RUN), BF),),
-        in_specs=[anym, anym, anym, anym, anym, pl.BlockSpec(memory_space=pltpu.SMEM)],
+        out_shape=(shape(y.shape, F32), shape(wy.shape, F32), shape(wx.shape, BF), shape(iy.shape, jnp.int32), shape(iy.shape, jnp.int32), shape((SAMPLES // RUN, 160, RUN), BF)),
+        in_specs=[anym] * 5 + [pl.BlockSpec(memory_space=pltpu.SMEM)],
         out_specs=(vm,) * 6,
-        scratch_shapes=[pltpu.VMEM(v.shape, v.dtype) for v in raw + (iy,)] + sort_scratch() + [dma((5,)), dma((5,)), dma((5,))],
+        scratch_shapes=[pltpu.VMEM(v.shape, v.dtype) for v in (y, wy, wx, iy, ix)] + [pltpu.VMEM(wx.shape, BF)] + sort_scratch() + [dma((5,)), dma((4,)), dma((4,))],
         compiler_params=pltpu.CompilerParams(vmem_limit_bytes=12 * 2**20, collective_id=1, has_side_effects=True),
         cost_estimate=pl.CostEstimate(flops=10**9, bytes_accessed=10**6, transcendentals=0),
         name='exchange',
     )(y, wy, wx, iy, ix, n)
 
 
-def spread_kernel(y_ref, wy_ref, wx_ref, iy_ref, ix_ref, d_own, n_ref, g_ref, e_ref, d_nb, pay, oh, rank, pt, acc, a_buf, b_buf):
+def spread_kernel(y_ref, wy_ref, wx_ref, key_ref, key_own, d_own, g_ref, e_ref, d_nb, pay, oh, rank, pt, acc, a_buf, b_buf):
     zero = jnp.zeros((16, RUN), BF)
 
     def run(d_ref, s):
@@ -174,7 +184,7 @@
                 acc[q, rows, :] += prod[16 * WIN * q:16 * WIN * (q + 1)]
 
     def block(o, d_ref, n_runs):
-        acc[...] = jnp.zeros_like(acc)
+        acc[:, :1056] = jnp.zeros((2, 1056, GRID), F32)
 
         @pl.loop(0, n_runs)
         def _(s):
@@ -185,10 +195,9 @@
             e_ref[o, q, 32:64] = acc[q, 1024:1056, :]
             g_ref[o, :, GRID * q:GRID * (q + 1)] = acc[q, 16:1040, :].astype(BF)
 
-    n_own = (n_ref[0] + (RUN - 1)) // RUN
-    n_nb = (jnp.sum(jnp.where(iy_ref[...] >= 0, 1.0, 0.0)).astype(jnp.int32) + (RUN - 1)) // RUN
-    payload(y_ref, wy_ref, wx_ref, iy_ref, ix_ref, pay)
-    ranks(iy_ref, oh, rank)
+    n_own, n_nb = [(jnp.sum(jnp.where(k[...] >= 0, 1.0, 0.0)).astype(jnp.int32) + (RUN - 1)) // RUN for k in (key_own, key_ref)]
+    payload(y_ref, wy_ref, wx_ref, key_ref, pay)
+    ranks(key_ref, oh, rank)
 
     @pl.loop(0, n_nb)
     def _(s):
@@ -198,12 +207,12 @@
     block(1, d_nb, n_nb)
 
 
-def spread(y, wy, wx, iy, ix, d_own, n):
+def spread(y, wy, wx, key, key_own, d_own):
     vm = pl.BlockSpec(memory_space=pltpu.VMEM)
     return pl.pallas_call(
         spread_kernel,
         out_shape=(jax.ShapeDtypeStruct((2, 1024, 2 * GRID), BF), jax.ShapeDtypeStruct((2, 2, 64, GRID), F32)),
-        in_specs=[vm, vm, vm, vm, vm, vm, pl.BlockSpec(memory_space=pltpu.SMEM)],
+        in_specs=[vm] * 6,
         out_specs=(vm, vm),
         scratch_shapes=[pltpu.VMEM((SAMPLES // RUN, 160, RUN), BF)] + sort_scratch() + [
             pltpu.VMEM((2, 16 * (66 + WIN), GRID), F32),
@@ -213,7 +222,7 @@
         compiler_params=pltpu.CompilerParams(vmem_limit_bytes=28 * 2**20),
         cost_estimate=pl.CostEstimate(flops=13 * 10**9, bytes_accessed=4 * 2**20, transcendentals=0),
         name='spread',
-    )(y, wy, wx, iy, ix, d_own, n)
+    )(y, wy, wx, key, key_own, d_own)
 
 
 def combine_kernel(gg, ee, tab, maps, dd, out_ref, hbuf, hs, ge, rx, s_all, part, rx2, scale,
@@ -259,12 +268,11 @@
         pi = lax.dot_general(lhs(1), t2, NT, preferred_element_type=F32)
         return pr[:, :128] - pi[:, 128:], pr[:, 128:] + pi[:, :128]
 
-    def transform(hc, o):
-        for k in range(2):
-            rows = slice(512 * k, 512 * k + 512)
-            pair = columns(hc, lambda q: gg[o, rows, GRID * q:GRID * (q + 1)])
-            for e in range(2):
-                hs[o, e, rows] = pair[e]
+    def transform(hc, o, k):
+        rows = slice(512 * k, 512 * k + 512)
+        pair = columns(hc, lambda q: gg[o, rows, GRID * q:GRID * (q + 1)])
+        for e in range(2):
+            hs[o, e, rows] = pair[e]
 
     def take_halos():
         for cp in e_copies:
@@ -279,15 +287,17 @@
         pair = columns(hc, lambda q: ge[:, GRID * q:GRID * (q + 1)])
         return pair
 
-    h_copies = [[remote(hbuf.at[hc, blocks[o]], hbuf.at[hc, blocks[o]], hsend.at[hc, o], hrecv.at[hc, o], sib) for o in range(2)] for hc in range(2)]
-
-    def send(hc, o, pair):
+    def piece(hc, o, k):
+        return remote(hbuf.at[hc, blocks[o], :, pl.ds(128 * k, 128)], hbuf.at[hc, blocks[o], :, pl.ds(128 * k, 128)], hsend.at[hc, o, k], hrecv.at[hc, o, k], sib)
+
+    h_copies = [[piece(hc, o, k) for o in range(2) for k in range(2)] for hc in range(2)]
+
+    def send(hc, o, k, pair):
         for e in range(2):
-            for end in range(2):
-                hs[o, e, 1008 * end:1008 * end + 16] = pair[e][32 * o + 16 * end:32 * o + 16 * end + 16]
+            hs[o, e, 1008 * k:1008 * k + 16] = pair[e][32 * o + 16 * k:32 * o + 16 * k + 16]
             for c in range(4):
-                hbuf[hc, blocks[o], e, :, 128 * c:128 * c + 128] = hs[o, e, pl.ds(c, 256, stride=4), :].astype(BF)
-        h_copies[hc][o].start()
+                hbuf[hc, blocks[o], e, 128 * k:128 * k + 128, 128 * c:128 * c + 128] = hs[o, e, pl.ds(512 * k + c, 128, stride=4), :].astype(BF)
+        h_copies[hc][2 * o + k].start()
 
     def image(hc):
         first = 256 * (y_id + (1 - 2 * y_id) * (core + hc - 2 * core * hc))
@@ -317,25 +327,30 @@
 
     y_copies = [remote(part.at[1 - core, :, pl.ds(128 * k, 128)], rx2.at[:, pl.ds(128 * k, 128)], ysend.at[k], yrecv.at[k], mate) for k in range(2)]
 
-    transform(0, 0)
+    transform(0, 0, 0)
+    transform(0, 0, 1)
     take_halos()
     pair = patch(0)
-    send(0, 0, pair)
-    transform(0, 1)
-    send(0, 1, pair)
-    transform(1, 0)
+    send(0, 0, 0, pair)
+    send(0, 0, 1, pair)
+    for k in range(2):
+        transform(0, 1, k)
+        send(0, 1, k, pair)
     pair = patch(1)
-    send(1, 0, pair)
+    for k in range(2):
+        transform(1, 0, k)
+        send(1, 0, k, pair)
     s_copy.wait()
     s_send.wait_send()
     s_recv.wait_recv()
-    for o in range(2):
-        h_copies[0][o].wait()
+    for cp in h_copies[0]:
+        cp.wait()
     image(0)
-    transform(1, 1)
-    send(1, 1, pair)
-    for o in range(2):
-        h_copies[1][o].wait()
+    for k in range(2):
+        transform(1, 1, k)
+        send(1, 1, k, pair)
+    for cp in h_copies[1]:
+        cp.wait()
     image(1)
     for k in range(2):
         y_copies[k].wait()
@@ -361,7 +376,7 @@
             pltpu.VMEM((2, 2, 256, 128), F32),
             pltpu.VMEM((2, 256, 128), F32),
             pltpu.VMEM((256, 128), F32),
-            dma((4,)), dma((2, 2)), dma((3,)), dma((2, 2)), dma((2, 2)), dma((2,)), dma((2,)),
+            dma((4,)), dma((2, 2)), dma((3,)), dma((2, 2, 2)), dma((2, 2, 2)), dma((2,)), dma((2,)),
         ],
         compiler_params=pltpu.CompilerParams(vmem_limit_bytes=24 * 2**20, collective_id=0, has_side_effects=True),
         cost_estimate=pl.CostEstimate(flops=7 * 10**9, bytes_accessed=12 * 2**20, transcendentals=0),
@@ -375,7 +390,7 @@
         hbm = [pltpu.with_memory_space_constraint(v, pltpu.HBM) for v in (kspace, weight_row, weight_col, grid_row[None], grid_col[None])]
         stacked = exchange(*hbm, valid_count)
         tab = jnp.asarray(tables(n_img))
-        gg, ee = spread(*stacked, valid_count)
+        gg, ee = spread(*stacked)
         return combine(gg, ee, tab, coil_maps, deapod[None])
 
     spec_samples = P(None, 'coil', ('slab', 'rows'))

time: 43.6 us -> 42.5 us (0.975)
  Pallas kernels: 42 us -> 41.2 us
    pallas_call x1, Pallas kernels: 9.44 us -> 8.91 us  [exchange(): pl.pallas_call(exchange_kernel, out_shape=(shape(y.shape, F32), shape(wy....]
    pallas_call x1, Pallas kernels: 16.6 us -> 16.1 us  [spread(): pl.pallas_call(spread_kernel, out_shape=(jax.ShapeDtypeStruct((2, 1024, 2...]
where the time goes in v5:
time: 42.5 us; the launch traced here: 42.7 us
  Pallas kernels  41.2 us (97%)
  local copies, waits for them, and re-layouts  0.72 us (2%)
  between operations  0.72 us (2%)
    pallas_call x1, Pallas kernels, combine(): pl.pallas_call(combine_kernel, out_shape=jax.ShapeDtypeStruct((2, 256, 12...  16.3 us
    pallas_call x1, Pallas kernels, spread(): pl.pallas_call(spread_kernel, out_shape=(jax.ShapeDtypeStruct((2, 1024, 2...  16.1 us
    pallas_call x1, Pallas kernels, exchange(): pl.pallas_call(exchange_kernel, out_shape=(shape(y.shape, F32), shape(wy....  8.91 us

profile of v5, /device:TPU:0, one launch (start us, length us, event | category | flops | bytes accessed | tf_op | source)
XLA Modules:
  0.0 42.7 jit_solution(4283589068904296254)
XLA Ops:
  0.7 8.9 %exchange.1 = (f32[2,4,2048]{2,1,0:T(4,128)S(1)}, f32[6,2048]{1,0:T(8,128)S(1)}, bf16[6,2048]{1,0:T(8,128)(2,1)S(1)}, s32[1,2048]{1,0:T(1,128)S(1)}, s32[1,2048]...) custom-call(f32[2,4,2048]{2,1,0:T(4,128)} %y_ref.1, f32[6,2048]{1,0:T(8,128)} %wy_ref.1, f32[6,2048]{1,0:T(8,128)} %wx_ref.1, ...), custom_call_target="tpu_custom_call" | custom-call | flops 1000000000 | bytes 1000000 | tf_op jit(solution)/shard_map/exchange/pallas_call | solution.py:149
  9.6 0.0 copy-start
  9.6 0.0 copy-start.1
  9.6 0.0 copy-start.2
  9.6 16.1 %spread.1 = (bf16[2,1024,2048]{2,1,0:T(8,128)(2,1)S(1)}, f32[2,2,64,1024]{3,2,1,0:T(8,128)S(1)}) custom-call(f32[2,4,2048]{2,1,0:T(4,128)S(1)} %get-tuple-element.13.y_ref, f32[6,2048]{1,0:T(8,128)S(1)} %get-tuple-element.14.wy_ref, bf16[6,2048]{1,0:T(8,128)(2,1)S(1)} %get-tuple-element.15.wx_ref, s32[1,2048]{1,0:T(1,128)S(1)} %get-tuple-element.16.key_ref, ...), custom_call_target="tpu_custom_call" | custom-call | flops 12999999488 | bytes 4194304 | tf_op jit(solution)/shard_map/spread/pallas_call | solution.py:212
  25.7 0.0 copy-done
  25.7 0.0 copy-done.1
  25.7 0.0 copy-done.2
  25.7 16.3 %combine.1 = f32[2,256,128]{2,1,0:T(8,128)S(1)} custom-call(bf16[2,1024,2048]{2,1,0:T(8,128)(2,1)S(1)} %get-tuple-element.19.gg, f32[2,2,64,1024]{3,2,1,0:T(8,128)S(1)} %get-tuple-element.20.ee, bf16[2,512,1024]{2,1,0:T(8,128)(2,1)S(1)} %copy-done.2, f32[2,4,512,128]{3,2,1,0:T(8,128)S(1)} %copy-done, f32[1,512]{1,0:T(1,128)S(1)} %bitcast.3), custom_call_target="tpu_custom_call" | custom-call | flops 7000000000 | bytes 12582912 | tf_op jit(solution)/shard_map/combine/pallas_call | solution.py:365
  42.0 0.7 %copy.12 = f32[2,256,128]{2,1,0:T(8,128)} copy(f32[2,256,128]{2,1,0:T(8,128)S(1)} %combine.1) | data formatting | bytes 524288
Async XLA Ops:
  9.6 16.1 %copy-start = (f32[2,4,512,128]{3,2,1,0:T(8,128)S(1)}, f32[2,4,512,128]{3,2,1,0:T(8,128)}, u32[]{:S(2)}) copy-start(f32[2,4,512,128]{3,2,1,0:T(8,128)} %maps.1) | copy-start | bytes 6291460
  9.6 16.1 %copy-start.1 = (f32[512]{0:T(512)S(1)}, f32[512]{0:T(512)}, u32[]{:S(2)}) copy-start(f32[512]{0:T(512)} %param.16) | copy-start | bytes 6148
  9.6 16.1 %copy-start.2 = (bf16[2,512,1024]{2,1,0:T(8,128)(2,1)S(1)}, bf16[2,512,1024]{2,1,0:T(8,128)(2,1)}, u32[]{:S(2)}) copy-start(bf16[2,512,1024]{2,1,0:T(8,128)(2,1)} %constant.2.clone.tab) | copy-start | bytes 6291460

commit v6 on v5

--- a/solution.py
+++ b/solution.py
@@ -62,48 +62,62 @@
     return lax.broadcasted_iota(jnp.int32, (16, 1), 0).astype(F32)
 
 
+def tiles(ch):
+    first = 4 * (ch // 2) + ch % 2
+    return first, first + 2
+
+
 def ranks(key_ref, oh, rank):
-    n_run = SAMPLES // RUN
-    for ch in range(n_run):
-        lanes = slice(RUN * ch, RUN * ch + RUN)
-        bucket = jnp.broadcast_to((((key_ref[:, lanes] >> 10) + 1) >> 2).astype(F32), (16, RUN)).astype(BF)
-        for g in range(5):
-            oh[80 * ch + 16 * g:80 * ch + 16 * g + 16, :] = jnp.where(bucket == (iota16() + 16 * g).astype(BF), jnp.ones((), BF), jnp.zeros((), BF))
+    n_chunk = SAMPLES // RUN
+    one, zero = jnp.ones((), BF), jnp.zeros((), BF)
+    for ch in range(n_chunk):
+        for k, t in enumerate(tiles(ch)):
+            bucket = jnp.broadcast_to((((key_ref[:, 128 * t:128 * t + 128] >> 10) + 1) >> 2).astype(F32), (16, 128)).astype(BF)
+            for g in range(5):
+                oh[80 * ch + 16 * g:80 * ch + 16 * g + 16, 128 * k:128 * k + 128] = jnp.where(bucket == (iota16() + 16 * g).astype(BF), one, zero)
     lower = lax.broadcasted_iota(jnp.int32, (RUN, RUN + 128), 0)
     upper = lax.broadcasted_iota(jnp.int32, (RUN, RUN + 128), 1)
     tri = jnp.where((lower < upper) | (upper >= RUN), 1.0, 0.0).astype(BF)
     pre = jnp.dot(oh[...], tri, preferred_element_type=F32)
-    counts = [pre[80 * ch:80 * ch + 80, RUN:] for ch in range(n_run)]
-    total = counts[0]
-    for ch in range(1, n_run):
-        total = total + counts[ch]
-    high = jnp.floor(total * (1.0 / 256.0))
-    low = total - 256.0 * high
+    counts = [pre[80 * ch:80 * ch + 80, RUN:] for ch in range(n_chunk)]
     strict = jnp.where(lax.broadcasted_iota(jnp.int32, (80, 80), 1) < lax.broadcasted_iota(jnp.int32, (80, 80), 0), 1.0, 0.0).astype(BF)
-    base = 256.0 * jnp.dot(strict, high.astype(BF), preferred_element_type=F32) + jnp.dot(strict, low.astype(BF), preferred_element_type=F32)
-    for ch in range(n_run):
-        lanes = slice(RUN * ch, RUN * ch + RUN)
-        place = pre[80 * ch:80 * ch + 80, :RUN] + jnp.concatenate([base] * (RUN // 128), axis=1)
-        place = jnp.sum(oh[80 * ch:80 * ch + 80, :].astype(F32) * place, axis=0, keepdims=True)
-        place = jnp.where(key_ref[:, lanes] >= 0, place, -1.0)
-        for k in range(RUN // 128):
-            rank[RUN * ch + 128 * k:RUN * ch + 128 * k + 128, :] = jnp.broadcast_to(place[:, 128 * k:128 * k + 128], (128, 128)).T
-        base = base + counts[ch]
-
-
-def reorder(s, pay, rank, pt):
+    for h in range(2):
+        total = counts[h]
+        for ch in range(h + 2, n_chunk, 2):
+            total = total + counts[ch]
+        high = jnp.floor(total * (1.0 / 256.0))
+        low = total - 256.0 * high
+        base = 256.0 * jnp.dot(strict, high.astype(BF), preferred_element_type=F32) + jnp.dot(strict, low.astype(BF), preferred_element_type=F32)
+        for ch in range(h, n_chunk, 2):
+            for k, t in enumerate(tiles(ch)):
+                place = pre[80 * ch:80 * ch + 80, 128 * k:128 * k + 128] + base
+                place = jnp.sum(oh[80 * ch:80 * ch + 80, 128 * k:128 * k + 128].astype(F32) * place, axis=0, keepdims=True)
+                place = jnp.where(key_ref[:, 128 * t:128 * t + 128] >= 0, place, -1.0)
+                rank[128 * t:128 * t + 128, :] = jnp.broadcast_to(place, (128, 128)).T
+            base = base + counts[ch]
+
+
+def reorder(sp, pay, rank, d_ref):
     lane = lax.broadcasted_iota(jnp.int32, (1, 128), 1).astype(F32)
     one, zero = jnp.ones((), BF), jnp.zeros((), BF)
-    for t in range(SAMPLES // 128):
-        rows = slice(128 * t, 128 * t + 128)
-        place = (rank[rows, :] - (s * RUN).astype(F32)).astype(BF)
-        for k in range(RUN // 128):
-            pt[rows, 128 * k:128 * k + 128] = jnp.where(place == (lane + 128 * k).astype(BF), one, zero)
-    return jnp.dot(pay[...], pt[...], preferred_element_type=F32).astype(BF)
+    for h in range(2):
+        total = None
+        for ch in range(h, SAMPLES // RUN, 2):
+            rows = []
+            for t in tiles(ch):
+                place = (rank[128 * t:128 * t + 128, :] - (sp * 256).astype(F32)).astype(BF)
+                rows.append(jnp.concatenate([jnp.where(place == (lane + 128 * k).astype(BF), one, zero) for k in range(2)], axis=1))
+            block = jnp.concatenate(rows, axis=0)
+            values = jnp.concatenate([pay[:, 128 * t:128 * t + 128] for t in tiles(ch)], axis=1)
+            part = jnp.dot(values, block, preferred_element_type=F32)
+            total = part if total is None else total + part
+        total = total.astype(BF)
+        for k in range(2):
+            d_ref[2 * sp + k, :, 128 * h:128 * h + 128] = total[:, 128 * k:128 * k + 128]
 
 
 def exchange_kernel(y_ref, wy_ref, wx_ref, iy_ref, ix_ref, n_ref, y_out, wy_out, wx_out, key_out, key_own, d_out,
-                    y_in, wy_in, wx_in, iy_in, ix_in, wx_bf, pay, oh, rank, pt, loc, ssem, rsem):
+                    y_in, wy_in, wx_in, iy_in, ix_in, wx_bf, pay, oh, rank, loc, ssem, rsem):
     row_id = lax.axis_index('rows')
     other = {'rows': (row_id + 2) % 4}
     barrier = pltpu.get_barrier_semaphore()
@@ -129,16 +143,16 @@
     payload(y_in, wy_in, wx_bf, key_own, pay)
     ranks(key_own, oh, rank)
 
-    @pl.loop(0, SAMPLES // RUN)
-    def _(s):
-        d_out[s] = reorder(s, pay, rank, pt)
+    @pl.loop(0, SAMPLES // RUN // 2)
+    def _(sp):
+        reorder(sp, pay, rank, d_out)
 
     for cp in sends:
         cp.wait()
 
 
 def sort_scratch():
-    return [pltpu.VMEM((160, SAMPLES), BF), pltpu.VMEM((80 * (SAMPLES // RUN), RUN), BF), pltpu.VMEM((SAMPLES, 128), F32), pltpu.VMEM((SAMPLES, RUN), BF)]
+    return [pltpu.VMEM((160, SAMPLES), BF), pltpu.VMEM((80 * (SAMPLES // RUN), RUN), BF), pltpu.VMEM((SAMPLES, 128), F32)]
 
 
 def exchange(y, wy, wx, iy, ix, n):
@@ -158,30 +172,35 @@
     )(y, wy, wx, iy, ix, n)
 
 
-def spread_kernel(y_ref, wy_ref, wx_ref, key_ref, key_own, d_own, g_ref, e_ref, d_nb, pay, oh, rank, pt, acc, a_buf, b_buf):
+def spread_kernel(y_ref, wy_ref, wx_ref, key_ref, key_own, d_own, g_ref, e_ref, d_nb, pay, oh, rank, acc, b_buf):
     zero = jnp.zeros((16, RUN), BF)
 
+    def window(d_ref, s, g0, right):
+        rel = (d_ref[s, 128:144, :].astype(F32) - (g0 + 1).astype(F32)).astype(BF)
+        left = []
+        for q in range(2):
+            e = [d_ref[s, 48 * q + 16 * j:48 * q + 16 * j + 16, :] for j in range(3)]
+            for gi in range(WIN):
+                m = [rel == jnp.array(gi - j, BF) for j in range(3)]
+                left.append(jnp.where(m[0], e[0], jnp.where(m[1], e[1], jnp.where(m[2], e[2], zero))))
+        prod = lax.dot_general(jnp.concatenate(left, axis=0), right, NT, preferred_element_type=F32)
+        rows = pl.ds(pl.multiple_of(g0 * 16, 16), 16 * WIN)
+        for q in range(2):
+            acc[q, rows, :] += prod[16 * WIN * q:16 * WIN * (q + 1)]
+
     def run(d_ref, s):
-        first = jnp.sum(jnp.where(lax.broadcasted_iota(jnp.int32, (1, RUN), 1) == 0, d_ref[s, 128:129, :].astype(F32), 0.0)).astype(jnp.int32) - 1
-        last = jnp.max(d_ref[s, 128:129, :].astype(F32)).astype(jnp.int32) + 1
+        number = d_ref[s, 128:129, :].astype(F32)
+        first = jnp.min(jnp.where(number > 0.0, number, 999.0)).astype(jnp.int32) - 1
+        last = jnp.max(number).astype(jnp.int32) + 1
         uc = d_ref[s, 144:160, :]
         eb = [d_ref[s, 96 + 16 * j:112 + 16 * j, :] for j in range(2)]
-        for g in range(64):
-            b_buf[16 * g:16 * g + 16, :] = jnp.where(uc == jnp.array(g, BF), eb[0], jnp.where(uc == jnp.array((g - 1) % 64, BF), eb[1], zero))
-
-        @pl.loop(0, (last - first + WIN) // WIN)
+        right = jnp.concatenate([jnp.where(uc == jnp.array(g, BF), eb[0], jnp.where(uc == jnp.array((g - 1) % 64, BF), eb[1], zero)) for g in range(64)], axis=0)
+        b_buf[...] = right
+        window(d_ref, s, first, right)
+
+        @pl.loop(1, (last - first + WIN) // WIN)
         def _(w):
-            g0 = first + WIN * w
-            rel = (d_ref[s, 128:144, :].astype(F32) - (g0 + 1).astype(F32)).astype(BF)
-            for gi in range(WIN):
-                m = [rel == jnp.array(gi - j, BF) for j in range(3)]
-                for q in range(2):
-                    e = [d_ref[s, 48 * q + 16 * j:48 * q + 16 * j + 16, :] for j in range(3)]
-                    a_buf[16 * (WIN * q + gi):16 * (WIN * q + gi) + 16, :] = jnp.where(m[0], e[0], jnp.where(m[1], e[1], jnp.where(m[2], e[2], zero)))
-            prod = lax.dot_general(a_buf[...], b_buf[...], NT, preferred_element_type=F32)
-            rows = pl.ds(pl.multiple_of(g0 * 16, 16), 16 * WIN)
-            for q in range(2):
-                acc[q, rows, :] += prod[16 * WIN * q:16 * WIN * (q + 1)]
+            window(d_ref, s, first + WIN * w, b_buf[...])
 
     def block(o, d_ref, n_runs):
         acc[:, :1056] = jnp.zeros((2, 1056, GRID), F32)
@@ -199,9 +218,9 @@
     payload(y_ref, wy_ref, wx_ref, key_ref, pay)
     ranks(key_ref, oh, rank)
 
-    @pl.loop(0, n_nb)
-    def _(s):
-        d_nb[s] = reorder(s, pay, rank, pt)
+    @pl.loop(0, (n_nb + 1) // 2)
+    def _(sp):
+        reorder(sp, pay, rank, d_nb)
 
     block(0, d_own, n_own)
     block(1, d_nb, n_nb)
@@ -216,7 +235,6 @@
         out_specs=(vm, vm),
         scratch_shapes=[pltpu.VMEM((SAMPLES // RUN, 160, RUN), BF)] + sort_scratch() + [
             pltpu.VMEM((2, 16 * (66 + WIN), GRID), F32),
-            pltpu.VMEM((32 * WIN, RUN), BF),
             pltpu.VMEM((GRID, RUN), BF),
         ],
         compiler_params=pltpu.CompilerParams(vmem_limit_bytes=28 * 2**20),

time: 42.5 us -> 39.2 us (0.922); the launches traced: 42.7 us -> 38.5 us
  Pallas kernels: 41.2 us -> 37.1 us
    pallas_call x1, Pallas kernels: 16.1 us -> 12.7 us  [spread(): pl.pallas_call(spread_kernel, out_shape=(jax.ShapeDtypeStruct((2, 1024, 2...]
    pallas_call x1, Pallas kernels: 8.91 us -> 7.85 us  [exchange(): pl.pallas_call(exchange_kernel, out_shape=(shape(y.shape, F32), shape(wy....]
where the time goes in v6:
time: 39.2 us; the launch traced here: 38.5 us
  Pallas kernels  37.1 us (95%)
  local copies, waits for them, and re-layouts  0.72 us (2%)
  between operations  0.72 us (2%)
    pallas_call x1, Pallas kernels, combine(): pl.pallas_call(combine_kernel, out_shape=jax.ShapeDtypeStruct((2, 256, 12...  16.5 us
    pallas_call x1, Pallas kernels, spread(): pl.pallas_call(spread_kernel, out_shape=(jax.ShapeDtypeStruct((2, 1024, 2...  12.7 us
    pallas_call x1, Pallas kernels, exchange(): pl.pallas_call(exchange_kernel, out_shape=(shape(y.shape, F32), shape(wy....  7.85 us

profile of v6, /device:TPU:0, one launch (start us, length us, event | category | flops | bytes accessed | tf_op | source)
XLA Modules:
  0.0 38.5 jit_solution(6686503498985115772)
XLA Ops:
  0.7 7.9 %exchange.1 = (f32[2,4,2048]{2,1,0:T(4,128)S(1)}, f32[6,2048]{1,0:T(8,128)S(1)}, bf16[6,2048]{1,0:T(8,128)(2,1)S(1)}, s32[1,2048]{1,0:T(1,128)S(1)}, s32[1,2048]...) custom-call(f32[2,4,2048]{2,1,0:T(4,128)} %y_ref.1, f32[6,2048]{1,0:T(8,128)} %wy_ref.1, f32[6,2048]{1,0:T(8,128)} %wx_ref.1, ...), custom_call_target="tpu_custom_call" | custom-call | flops 1000000000 | bytes 1000000 | tf_op jit(solution)/shard_map/exchange/pallas_call | solution.py:163
  8.5 0.0 copy-start
  8.5 0.0 copy-start.1
  8.5 0.0 copy-start.2
  8.5 12.7 %spread.1 = (bf16[2,1024,2048]{2,1,0:T(8,128)(2,1)S(1)}, f32[2,2,64,1024]{3,2,1,0:T(8,128)S(1)}) custom-call(f32[2,4,2048]{2,1,0:T(4,128)S(1)} %get-tuple-element.13.y_ref, f32[6,2048]{1,0:T(8,128)S(1)} %get-tuple-element.14.wy_ref, bf16[6,2048]{1,0:T(8,128)(2,1)S(1)} %get-tuple-element.15.wx_ref, s32[1,2048]{1,0:T(1,128)S(1)} %get-tuple-element.16.key_ref, ...), custom_call_target="tpu_custom_call" | custom-call | flops 12999999488 | bytes 4194304 | tf_op jit(solution)/shard_map/spread/pallas_call | solution.py:231
  21.3 0.0 copy-done
  21.3 0.0 copy-done.1
  21.3 0.0 copy-done.2
  21.3 16.5 %combine.1 = f32[2,256,128]{2,1,0:T(8,128)S(1)} custom-call(bf16[2,1024,2048]{2,1,0:T(8,128)(2,1)S(1)} %get-tuple-element.19.gg, f32[2,2,64,1024]{3,2,1,0:T(8,128)S(1)} %get-tuple-element.20.ee, bf16[2,512,1024]{2,1,0:T(8,128)(2,1)S(1)} %copy-done.2, f32[2,4,512,128]{3,2,1,0:T(8,128)S(1)} %copy-done, f32[1,512]{1,0:T(1,128)S(1)} %bitcast.3), custom_call_target="tpu_custom_call" | custom-call | flops 7000000000 | bytes 12582912 | tf_op jit(solution)/shard_map/combine/pallas_call | solution.py:383
  37.8 0.7 %copy.12 = f32[2,256,128]{2,1,0:T(8,128)} copy(f32[2,256,128]{2,1,0:T(8,128)S(1)} %combine.1) | data formatting | bytes 524288
Async XLA Ops:
  8.5 12.8 %copy-start = (f32[2,4,512,128]{3,2,1,0:T(8,128)S(1)}, f32[2,4,512,128]{3,2,1,0:T(8,128)}, u32[]{:S(2)}) copy-start(f32[2,4,512,128]{3,2,1,0:T(8,128)} %maps.1) | copy-start | bytes 6291460
  8.5 12.8 %copy-start.1 = (f32[512]{0:T(512)S(1)}, f32[512]{0:T(512)}, u32[]{:S(2)}) copy-start(f32[512]{0:T(512)} %param.16) | copy-start | bytes 6148
  8.5 12.8 %copy-start.2 = (bf16[2,512,1024]{2,1,0:T(8,128)(2,1)S(1)}, bf16[2,512,1024]{2,1,0:T(8,128)(2,1)}, u32[]{:S(2)}) copy-start(bf16[2,512,1024]{2,1,0:T(8,128)(2,1)} %constant.2.clone.tab) | copy-start | bytes 6291460
